TPU v7x, 32 devices: a 4x4x1 block of a 4x4x8 slice. The times are simulated.
32 devices in a mesh: dp: 1 (over z), tp: 4 (over y), pp: 8 (over x, core).
Axes of the slice: x: 4, y: 4, z: 1, core: 2. Of those that a mesh axis runs over, the one named last changes fastest.
The devices are a block of a 4x4x8 slice.
Arguments:
- tokens_in: bfloat16 [8, 128, 1024], P('dp')
- targets: bfloat16 [8, 128, 1024], P('dp')
- w_in: bfloat16 [8, 2, 1024, 4096], P('pp', None, None, 'tp')
- w_out: bfloat16 [8, 2, 4096, 1024], P('pp', None, 'tp')
Outputs:
- output 1: float32 [8, 2, 1024, 4096], P(('dp', 'pp'), None, None, 'tp')
- output 2: float32 [8, 2, 4096, 1024], P(('dp', 'pp'), None, 'tp')
- output 3: float32 [1], P('dp')
All inputs are finite; a program needn't handle non-finite values.
Results may differ from a plain program's by a relative error of at most 0.0120252.
Values are sent between devices in bfloat16 or wider.
A program may use at most 768 MiB of HBM per device.

v0:
```python
import jax
import jax.numpy as jnp
from jax import lax
from jax.sharding import PartitionSpec as P


def gelu_back(pre_act, back_grad):
    gelu_pull = jax.vjp(jax.nn.gelu, pre_act.astype(jnp.float32))[1]
    return gelu_pull(back_grad)[0].astype(jnp.bfloat16)


def solution(mesh):
    n_stage = mesh.shape["pp"]
    fwd_pairs = [(src_idx, src_idx + 1) for src_idx in range(n_stage - 1)]
    bwd_pairs = [(src_idx + 1, src_idx) for src_idx in range(n_stage - 1)]

    def device_program(x_loc, y_loc, w_in, w_out):
        n_micro, n_tok, d_model = x_loc.shape
        hidden = w_in.shape[3]
        first_w = [w_in[0, layer_idx] for layer_idx in range(2)]
        second_w = [w_out[0, layer_idx] for layer_idx in range(2)]
        stage_idx = lax.axis_index("pp")
        is_first = stage_idx == 0
        is_last = stage_idx == n_stage - 1
        n_slots = min(n_micro, 2 * n_stage - 1)
        n_ticks = n_micro + 2 * n_stage - 2
        inv_count = 1.0 / (n_micro * n_tok * d_model)
        zero_act = jnp.zeros((n_tok, d_model), jnp.bfloat16)

        def run_tick(tick_idx, loop_state):
            recv_act, recv_grad, store_in, store_pre, store_post, acc_first, acc_second, loss_sum = loop_state
            store_in = list(store_in)
            store_pre = list(store_pre)
            store_post = list(store_post)
            acc_first = list(acc_first)
            acc_second = list(acc_second)
            m_fwd = tick_idx - stage_idx
            ok_fwd = (m_fwd >= 0) & (m_fwd < n_micro)
            m_fwd_c = jnp.clip(m_fwd, 0, n_micro - 1)
            slot_fwd = jnp.where(ok_fwd, m_fwd_c % n_slots, n_slots)
            x_first = lax.dynamic_index_in_dim(x_loc, m_fwd_c, 0, keepdims=False)
            cur_act = jnp.where(is_first, x_first, recv_act)
            for layer_idx in range(2):
                pre_act = jnp.einsum("bd,df->bf", cur_act, first_w[layer_idx], preferred_element_type=jnp.float32).astype(jnp.bfloat16)
                post_act = jax.nn.gelu(pre_act.astype(jnp.float32)).astype(jnp.bfloat16)
                part_out = jnp.einsum("bf,fd->bd", post_act, second_w[layer_idx], preferred_element_type=jnp.float32).astype(jnp.bfloat16)
                branch = lax.psum(part_out, "tp")
                store_in[layer_idx] = lax.dynamic_update_index_in_dim(store_in[layer_idx], cur_act, slot_fwd, 0)
                store_pre[layer_idx] = lax.dynamic_update_index_in_dim(store_pre[layer_idx], pre_act, slot_fwd, 0)
                store_post[layer_idx] = lax.dynamic_update_index_in_dim(store_post[layer_idx], post_act, slot_fwd, 0)
                cur_act = (cur_act.astype(jnp.float32) + branch.astype(jnp.float32)).astype(jnp.bfloat16)
            y_mb = lax.dynamic_index_in_dim(y_loc, m_fwd_c, 0, keepdims=False)
            error_val = cur_act.astype(jnp.float32) - y_mb.astype(jnp.float32)
            loss_sum = loss_sum + jnp.where(is_last & ok_fwd, 0.5 * jnp.sum(error_val * error_val), 0.0)
            m_bwd = tick_idx - (2 * n_stage - 2 - stage_idx)
            ok_bwd = (m_bwd >= 0) & (m_bwd < n_micro)
            slot_bwd = jnp.clip(m_bwd, 0, n_micro - 1) % n_slots
            cur_grad = jnp.where(is_last, (error_val * inv_count).astype(jnp.bfloat16), recv_grad)
            cur_grad = jnp.where(ok_bwd, cur_grad, zero_act)
            for layer_idx in (1, 0):
                act_sv = lax.dynamic_index_in_dim(store_in[layer_idx], slot_bwd, 0, keepdims=False)
                pre_sv = lax.dynamic_index_in_dim(store_pre[layer_idx], slot_bwd, 0, keepdims=False)
                post_sv = lax.dynamic_index_in_dim(store_post[layer_idx], slot_bwd, 0, keepdims=False)
                back_grad = jnp.einsum("bd,fd->bf", cur_grad, second_w[layer_idx], preferred_element_type=jnp.float32)
                gate_grad = gelu_back(pre_sv, back_grad)
                part_in = jnp.einsum("bf,df->bd", gate_grad, first_w[layer_idx], preferred_element_type=jnp.float32).astype(jnp.bfloat16)
                spread = lax.psum(part_in, "tp")
                acc_first[layer_idx] = acc_first[layer_idx] + jnp.einsum("bd,bf->df", act_sv, gate_grad, preferred_element_type=jnp.float32)
                acc_second[layer_idx] = acc_second[layer_idx] + jnp.einsum("bf,bd->fd", post_sv, cur_grad, preferred_element_type=jnp.float32)
                cur_grad = (cur_grad.astype(jnp.float32) + spread.astype(jnp.float32)).astype(jnp.bfloat16)
            recv_act = lax.ppermute(cur_act, "pp", fwd_pairs)
            recv_grad = lax.ppermute(cur_grad, "pp", bwd_pairs)
            return (recv_act, recv_grad, tuple(store_in), tuple(store_pre), tuple(store_post), tuple(acc_first), tuple(acc_second), loss_sum)

        buf_in = jnp.zeros((n_slots + 1, n_tok, d_model), jnp.bfloat16)
        buf_hidden = jnp.zeros((n_slots + 1, n_tok, hidden), jnp.bfloat16)
        zero_first = jnp.zeros((d_model, hidden), jnp.float32)
        zero_second = jnp.zeros((hidden, d_model), jnp.float32)
        init_state = (zero_act, zero_act, (buf_in, buf_in), (buf_hidden, buf_hidden), (buf_hidden, buf_hidden), (zero_first, zero_first), (zero_second, zero_second), jnp.zeros((), jnp.float32))
        final_state = lax.fori_loop(0, n_ticks, run_tick, init_state)
        grad_first = jnp.stack(final_state[5])[None]
        grad_second = jnp.stack(final_state[6])[None]
        loss_val = (lax.psum(final_state[7], "pp") * inv_count).reshape(1)
        return grad_first, grad_second, loss_val

    return jax.shard_map(
        device_program,
        mesh=mesh,
        in_specs=(P("dp", None, None), P("dp", None, None), P("pp", None, None, "tp"), P("pp", None, "tp", None)),
        out_specs=(P(("dp", "pp"), None, None, "tp"), P(("dp", "pp"), None, "tp", None), P("dp")),
        check_vma=False,
    )
```

profile of v0, /device:TPU:96, one launch (start us, length us, event | category | flops | bytes accessed | tf_op | source)
XLA Modules:
  0.0 4034.2 jit_solution(5385306353231253797)
XLA Ops:
  23.9 3969.1 %while.41 = (s32[]{:T(128)}, bf16[128,1024]{1,0:T(8,128)(2,1)}, bf16[128,1024]{1,0:T(8,128)(2,1)S(1)}, bf16[9,128,1024]{2,1,0:T(8,128)(2,1)}, bf16[9,128,1024]{2...) while((s32[]{:T(128)}, bf16[128,1024]{1,0:T(8,128)(2,1)}, ...), condition=%wide.region_6.7_spmd.clone, body=%wide.region_0.6_spmd.clone.sunk | while | flops 3250323456 | bytes 109317200 | solution.py:80
  28.5 39.4 all-reduce.5.cloned.1.call-done
  73.2 36.4 all-reduce.7.cloned.1.call-done
  164.4 33.6 all-reduce.11.cloned.1.call-done
  208.8 39.1 all-reduce.5.cloned.1.call-done
  253.2 36.4 all-reduce.7.cloned.1.call-done
  390.2 38.1 all-reduce.5.cloned.1.call-done
  433.6 36.4 all-reduce.7.cloned.1.call-done
  526.2 32.3 all-reduce.11.cloned.1.call-done
  570.6 38.1 all-reduce.5.cloned.1.call-done
  613.9 36.4 all-reduce.7.cloned.1.call-done
  750.9 38.1 all-reduce.5.cloned.1.call-done
  794.3 36.4 all-reduce.7.cloned.1.call-done
  931.3 38.1 all-reduce.5.cloned.1.call-done
  974.7 36.4 all-reduce.7.cloned.1.call-done
  1067.3 32.3 all-reduce.11.cloned.1.call-done
  1111.7 38.1 all-reduce.5.cloned.1.call-done
  1155.1 36.4 all-reduce.7.cloned.1.call-done
  1292.1 38.1 all-reduce.5.cloned.1.call-done
  1335.5 36.4 all-reduce.7.cloned.1.call-done
  1472.4 38.2 all-reduce.5.cloned.1.call-done
  1515.9 36.4 all-reduce.7.cloned.1.call-done
  1652.8 38.2 all-reduce.5.cloned.1.call-done
  1696.3 36.5 all-reduce.7.cloned.1.call-done
  1833.3 38.1 all-reduce.5.cloned.1.call-done
  1876.7 36.4 all-reduce.7.cloned.1.call-done
  2013.7 38.2 all-reduce.5.cloned.1.call-done
  2057.1 36.4 all-reduce.7.cloned.1.call-done
  2194.1 38.2 all-reduce.5.cloned.1.call-done
  2237.5 36.4 all-reduce.7.cloned.1.call-done
  2374.5 38.1 all-reduce.5.cloned.1.call-done
  2417.9 36.4 all-reduce.7.cloned.1.call-done
  2554.9 38.1 all-reduce.5.cloned.1.call-done
  2598.3 36.4 all-reduce.7.cloned.1.call-done
  2735.2 38.1 all-reduce.5.cloned.1.call-done
  2778.6 36.4 all-reduce.7.cloned.1.call-done
  2915.6 38.1 all-reduce.5.cloned.1.call-done
  2959.0 36.4 all-reduce.7.cloned.1.call-done
  3095.9 38.1 all-reduce.5.cloned.1.call-done
  3139.3 36.4 all-reduce.7.cloned.1.call-done
  3276.3 38.1 all-reduce.5.cloned.1.call-done
  3319.7 36.4 all-reduce.7.cloned.1.call-done
  3456.6 38.1 all-reduce.5.cloned.1.call-done
  3500.0 36.4 all-reduce.7.cloned.1.call-done
  3637.0 38.1 all-reduce.5.cloned.1.call-done
  3680.4 36.4 all-reduce.7.cloned.1.call-done
  3817.3 38.1 all-reduce.5.cloned.1.call-done
  3860.7 36.4 all-reduce.7.cloned.1.call-done
  (961 shorter events, 2258.6 us)
Async XLA Ops:
  28.4 81.2 %all-reduce.7.cloned.1.call-start = ((), (), s32[]{:S(2)}) async-start(), calls=%async_computation.1 | async-start | bytes 524288 | tf_op jit(solution)/shard_map/while/body/eval_jaxpr/psum | solution.py:47
  72.3 84.2 %all-reduce.9.cloned.1.call-start = ((), (), s32[]{:S(2)}) async-start(), calls=%async_computation.2 | async-start | bytes 524288 | tf_op jit(solution)/shard_map/while/body/eval_jaxpr/psum | solution.py:67
  111.6 92.5 %collective-permute-start = (bf16[128,1024]{1,0:T(8,128)(2,1)S(1)}, bf16[128,1024]{1,0:T(8,128)(2,1)}, u32[]{:S(2)}, u32[]{:S(2)}) collective-permute-start(bf16[128,1024]{1,0:T(8,128)(2,1)S(1)} %get-tuple-element.903), channel_id=1, source_target_pairs={{0,1},{1,2},{2,3},{3,4},{4,5},{5,6},{6,7},{8,9},{9,10},{10,11},{11... | collective-permute-start | bytes 786440 | tf_op jit(solution)/shard_map/while/body/eval_jaxpr/ppermute | solution.py:71
  208.8 80.9 %all-reduce.7.cloned.1.call-start = ((), (), s32[]{:S(2)}) async-start(), calls=%async_computation.1 | async-start | bytes 524288 | tf_op jit(solution)/shard_map/while/body/eval_jaxpr/psum | solution.py:47
  252.3 84.2 %all-reduce.9.cloned.1.call-start = ((), (), s32[]{:S(2)}) async-start(), calls=%async_computation.2 | async-start | bytes 524288 | tf_op jit(solution)/shard_map/while/body/eval_jaxpr/psum | solution.py:67
  291.7 93.9 %collective-permute-start = (bf16[128,1024]{1,0:T(8,128)(2,1)S(1)}, bf16[128,1024]{1,0:T(8,128)(2,1)}, u32[]{:S(2)}, u32[]{:S(2)}) collective-permute-start(bf16[128,1024]{1,0:T(8,128)(2,1)S(1)} %get-tuple-element.903), channel_id=1, source_target_pairs={{0,1},{1,2},{2,3},{3,4},{4,5},{5,6},{6,7},{8,9},{9,10},{10,11},{11... | collective-permute-start | bytes 786440 | tf_op jit(solution)/shard_map/while/body/eval_jaxpr/ppermute | solution.py:71
  432.7 84.2 %all-reduce.9.cloned.1.call-start = ((), (), s32[]{:S(2)}) async-start(), calls=%async_computation.2 | async-start | bytes 524288 | tf_op jit(solution)/shard_map/while/body/eval_jaxpr/psum | solution.py:67
  472.0 93.9 %collective-permute-start = (bf16[128,1024]{1,0:T(8,128)(2,1)S(1)}, bf16[128,1024]{1,0:T(8,128)(2,1)}, u32[]{:S(2)}, u32[]{:S(2)}) collective-permute-start(bf16[128,1024]{1,0:T(8,128)(2,1)S(1)} %get-tuple-element.903), channel_id=1, source_target_pairs={{0,1},{1,2},{2,3},{3,4},{4,5},{5,6},{6,7},{8,9},{9,10},{10,11},{11... | collective-permute-start | bytes 786440 | tf_op jit(solution)/shard_map/while/body/eval_jaxpr/ppermute | solution.py:71
  613.0 84.2 %all-reduce.9.cloned.1.call-start = ((), (), s32[]{:S(2)}) async-start(), calls=%async_computation.2 | async-start | bytes 524288 | tf_op jit(solution)/shard_map/while/body/eval_jaxpr/psum | solution.py:67
  652.4 93.9 %collective-permute-start = (bf16[128,1024]{1,0:T(8,128)(2,1)S(1)}, bf16[128,1024]{1,0:T(8,128)(2,1)}, u32[]{:S(2)}, u32[]{:S(2)}) collective-permute-start(bf16[128,1024]{1,0:T(8,128)(2,1)S(1)} %get-tuple-element.903), channel_id=1, source_target_pairs={{0,1},{1,2},{2,3},{3,4},{4,5},{5,6},{6,7},{8,9},{9,10},{10,11},{11... | collective-permute-start | bytes 786440 | tf_op jit(solution)/shard_map/while/body/eval_jaxpr/ppermute | solution.py:71
  793.4 84.2 %all-reduce.9.cloned.1.call-start = ((), (), s32[]{:S(2)}) async-start(), calls=%async_computation.2 | async-start | bytes 524288 | tf_op jit(solution)/shard_map/while/body/eval_jaxpr/psum | solution.py:67
  832.8 93.9 %collective-permute-start = (bf16[128,1024]{1,0:T(8,128)(2,1)S(1)}, bf16[128,1024]{1,0:T(8,128)(2,1)}, u32[]{:S(2)}, u32[]{:S(2)}) collective-permute-start(bf16[128,1024]{1,0:T(8,128)(2,1)S(1)} %get-tuple-element.903), channel_id=1, source_target_pairs={{0,1},{1,2},{2,3},{3,4},{4,5},{5,6},{6,7},{8,9},{9,10},{10,11},{11... | collective-permute-start | bytes 786440 | tf_op jit(solution)/shard_map/while/body/eval_jaxpr/ppermute | solution.py:71
  973.8 84.2 %all-reduce.9.cloned.1.call-start = ((), (), s32[]{:S(2)}) async-start(), calls=%async_computation.2 | async-start | bytes 524288 | tf_op jit(solution)/shard_map/while/body/eval_jaxpr/psum | solution.py:67
  1013.1 93.9 %collective-permute-start = (bf16[128,1024]{1,0:T(8,128)(2,1)S(1)}, bf16[128,1024]{1,0:T(8,128)(2,1)}, u32[]{:S(2)}, u32[]{:S(2)}) collective-permute-start(bf16[128,1024]{1,0:T(8,128)(2,1)S(1)} %get-tuple-element.903), channel_id=1, source_target_pairs={{0,1},{1,2},{2,3},{3,4},{4,5},{5,6},{6,7},{8,9},{9,10},{10,11},{11... | collective-permute-start | bytes 786440 | tf_op jit(solution)/shard_map/while/body/eval_jaxpr/ppermute | solution.py:71
  1154.2 84.2 %all-reduce.9.cloned.1.call-start = ((), (), s32[]{:S(2)}) async-start(), calls=%async_computation.2 | async-start | bytes 524288 | tf_op jit(solution)/shard_map/while/body/eval_jaxpr/psum | solution.py:67
  1193.5 93.9 %collective-permute-start = (bf16[128,1024]{1,0:T(8,128)(2,1)S(1)}, bf16[128,1024]{1,0:T(8,128)(2,1)}, u32[]{:S(2)}, u32[]{:S(2)}) collective-permute-start(bf16[128,1024]{1,0:T(8,128)(2,1)S(1)} %get-tuple-element.903), channel_id=1, source_target_pairs={{0,1},{1,2},{2,3},{3,4},{4,5},{5,6},{6,7},{8,9},{9,10},{10,11},{11... | collective-permute-start | bytes 786440 | tf_op jit(solution)/shard_map/while/body/eval_jaxpr/ppermute | solution.py:71
  1334.6 84.2 %all-reduce.9.cloned.1.call-start = ((), (), s32[]{:S(2)}) async-start(), calls=%async_computation.2 | async-start | bytes 524288 | tf_op jit(solution)/shard_map/while/body/eval_jaxpr/psum | solution.py:67
  1373.9 93.9 %collective-permute-start = (bf16[128,1024]{1,0:T(8,128)(2,1)S(1)}, bf16[128,1024]{1,0:T(8,128)(2,1)}, u32[]{:S(2)}, u32[]{:S(2)}) collective-permute-start(bf16[128,1024]{1,0:T(8,128)(2,1)S(1)} %get-tuple-element.903), channel_id=1, source_target_pairs={{0,1},{1,2},{2,3},{3,4},{4,5},{5,6},{6,7},{8,9},{9,10},{10,11},{11... | collective-permute-start | bytes 786440 | tf_op jit(solution)/shard_map/while/body/eval_jaxpr/ppermute | solution.py:71
  1515.0 84.2 %all-reduce.9.cloned.1.call-start = ((), (), s32[]{:S(2)}) async-start(), calls=%async_computation.2 | async-start | bytes 524288 | tf_op jit(solution)/shard_map/while/body/eval_jaxpr/psum | solution.py:67
  1554.3 93.9 %collective-permute-start = (bf16[128,1024]{1,0:T(8,128)(2,1)S(1)}, bf16[128,1024]{1,0:T(8,128)(2,1)}, u32[]{:S(2)}, u32[]{:S(2)}) collective-permute-start(bf16[128,1024]{1,0:T(8,128)(2,1)S(1)} %get-tuple-element.903), channel_id=1, source_target_pairs={{0,1},{1,2},{2,3},{3,4},{4,5},{5,6},{6,7},{8,9},{9,10},{10,11},{11... | collective-permute-start | bytes 786440 | tf_op jit(solution)/shard_map/while/body/eval_jaxpr/ppermute | solution.py:71
  1652.8 80.0 %all-reduce.7.cloned.1.call-start = ((), (), s32[]{:S(2)}) async-start(), calls=%async_computation.1 | async-start | bytes 524288 | tf_op jit(solution)/shard_map/while/body/eval_jaxpr/psum | solution.py:47
  1695.4 84.2 %all-reduce.9.cloned.1.call-start = ((), (), s32[]{:S(2)}) async-start(), calls=%async_computation.2 | async-start | bytes 524288 | tf_op jit(solution)/shard_map/while/body/eval_jaxpr/psum | solution.py:67
  1734.8 93.9 %collective-permute-start = (bf16[128,1024]{1,0:T(8,128)(2,1)S(1)}, bf16[128,1024]{1,0:T(8,128)(2,1)}, u32[]{:S(2)}, u32[]{:S(2)}) collective-permute-start(bf16[128,1024]{1,0:T(8,128)(2,1)S(1)} %get-tuple-element.903), channel_id=1, source_target_pairs={{0,1},{1,2},{2,3},{3,4},{4,5},{5,6},{6,7},{8,9},{9,10},{10,11},{11... | collective-permute-start | bytes 786440 | tf_op jit(solution)/shard_map/while/body/eval_jaxpr/ppermute | solution.py:71
  1875.8 84.2 %all-reduce.9.cloned.1.call-start = ((), (), s32[]{:S(2)}) async-start(), calls=%async_computation.2 | async-start | bytes 524288 | tf_op jit(solution)/shard_map/while/body/eval_jaxpr/psum | solution.py:67
  1915.2 93.9 %collective-permute-start = (bf16[128,1024]{1,0:T(8,128)(2,1)S(1)}, bf16[128,1024]{1,0:T(8,128)(2,1)}, u32[]{:S(2)}, u32[]{:S(2)}) collective-permute-start(bf16[128,1024]{1,0:T(8,128)(2,1)S(1)} %get-tuple-element.903), channel_id=1, source_target_pairs={{0,1},{1,2},{2,3},{3,4},{4,5},{5,6},{6,7},{8,9},{9,10},{10,11},{11... | collective-permute-start | bytes 786440 | tf_op jit(solution)/shard_map/while/body/eval_jaxpr/ppermute | solution.py:71
  2013.6 80.0 %all-reduce.7.cloned.1.call-start = ((), (), s32[]{:S(2)}) async-start(), calls=%async_computation.1 | async-start | bytes 524288 | tf_op jit(solution)/shard_map/while/body/eval_jaxpr/psum | solution.py:47
  2056.2 84.2 %all-reduce.9.cloned.1.call-start = ((), (), s32[]{:S(2)}) async-start(), calls=%async_computation.2 | async-start | bytes 524288 | tf_op jit(solution)/shard_map/while/body/eval_jaxpr/psum | solution.py:67
  2095.6 93.9 %collective-permute-start = (bf16[128,1024]{1,0:T(8,128)(2,1)S(1)}, bf16[128,1024]{1,0:T(8,128)(2,1)}, u32[]{:S(2)}, u32[]{:S(2)}) collective-permute-start(bf16[128,1024]{1,0:T(8,128)(2,1)S(1)} %get-tuple-element.903), channel_id=1, source_target_pairs={{0,1},{1,2},{2,3},{3,4},{4,5},{5,6},{6,7},{8,9},{9,10},{10,11},{11... | collective-permute-start | bytes 786440 | tf_op jit(solution)/shard_map/while/body/eval_jaxpr/ppermute | solution.py:71
  2236.7 84.2 %all-reduce.9.cloned.1.call-start = ((), (), s32[]{:S(2)}) async-start(), calls=%async_computation.2 | async-start | bytes 524288 | tf_op jit(solution)/shard_map/while/body/eval_jaxpr/psum | solution.py:67
  2276.0 93.9 %collective-permute-start = (bf16[128,1024]{1,0:T(8,128)(2,1)S(1)}, bf16[128,1024]{1,0:T(8,128)(2,1)}, u32[]{:S(2)}, u32[]{:S(2)}) collective-permute-start(bf16[128,1024]{1,0:T(8,128)(2,1)S(1)} %get-tuple-element.903), channel_id=1, source_target_pairs={{0,1},{1,2},{2,3},{3,4},{4,5},{5,6},{6,7},{8,9},{9,10},{10,11},{11... | collective-permute-start | bytes 786440 | tf_op jit(solution)/shard_map/while/body/eval_jaxpr/ppermute | solution.py:71
  2417.0 84.2 %all-reduce.9.cloned.1.call-start = ((), (), s32[]{:S(2)}) async-start(), calls=%async_computation.2 | async-start | bytes 524288 | tf_op jit(solution)/shard_map/while/body/eval_jaxpr/psum | solution.py:67
  2456.3 93.9 %collective-permute-start = (bf16[128,1024]{1,0:T(8,128)(2,1)S(1)}, bf16[128,1024]{1,0:T(8,128)(2,1)}, u32[]{:S(2)}, u32[]{:S(2)}) collective-permute-start(bf16[128,1024]{1,0:T(8,128)(2,1)S(1)} %get-tuple-element.903), channel_id=1, source_target_pairs={{0,1},{1,2},{2,3},{3,4},{4,5},{5,6},{6,7},{8,9},{9,10},{10,11},{11... | collective-permute-start | bytes 786440 | tf_op jit(solution)/shard_map/while/body/eval_jaxpr/ppermute | solution.py:71
  2597.4 84.2 %all-reduce.9.cloned.1.call-start = ((), (), s32[]{:S(2)}) async-start(), calls=%async_computation.2 | async-start | bytes 524288 | tf_op jit(solution)/shard_map/while/body/eval_jaxpr/psum | solution.py:67
  2636.7 93.9 %collective-permute-start = (bf16[128,1024]{1,0:T(8,128)(2,1)S(1)}, bf16[128,1024]{1,0:T(8,128)(2,1)}, u32[]{:S(2)}, u32[]{:S(2)}) collective-permute-start(bf16[128,1024]{1,0:T(8,128)(2,1)S(1)} %get-tuple-element.903), channel_id=1, source_target_pairs={{0,1},{1,2},{2,3},{3,4},{4,5},{5,6},{6,7},{8,9},{9,10},{10,11},{11... | collective-permute-start | bytes 786440 | tf_op jit(solution)/shard_map/while/body/eval_jaxpr/ppermute | solution.py:71
  2777.7 84.2 %all-reduce.9.cloned.1.call-start = ((), (), s32[]{:S(2)}) async-start(), calls=%async_computation.2 | async-start | bytes 524288 | tf_op jit(solution)/shard_map/while/body/eval_jaxpr/psum | solution.py:67
  2817.1 93.9 %collective-permute-start = (bf16[128,1024]{1,0:T(8,128)(2,1)S(1)}, bf16[128,1024]{1,0:T(8,128)(2,1)}, u32[]{:S(2)}, u32[]{:S(2)}) collective-permute-start(bf16[128,1024]{1,0:T(8,128)(2,1)S(1)} %get-tuple-element.903), channel_id=1, source_target_pairs={{0,1},{1,2},{2,3},{3,4},{4,5},{5,6},{6,7},{8,9},{9,10},{10,11},{11... | collective-permute-start | bytes 786440 | tf_op jit(solution)/shard_map/while/body/eval_jaxpr/ppermute | solution.py:71
  2958.1 84.2 %all-reduce.9.cloned.1.call-start = ((), (), s32[]{:S(2)}) async-start(), calls=%async_computation.2 | async-start | bytes 524288 | tf_op jit(solution)/shard_map/while/body/eval_jaxpr/psum | solution.py:67
  2997.4 93.9 %collective-permute-start = (bf16[128,1024]{1,0:T(8,128)(2,1)S(1)}, bf16[128,1024]{1,0:T(8,128)(2,1)}, u32[]{:S(2)}, u32[]{:S(2)}) collective-permute-start(bf16[128,1024]{1,0:T(8,128)(2,1)S(1)} %get-tuple-element.903), channel_id=1, source_target_pairs={{0,1},{1,2},{2,3},{3,4},{4,5},{5,6},{6,7},{8,9},{9,10},{10,11},{11... | collective-permute-start | bytes 786440 | tf_op jit(solution)/shard_map/while/body/eval_jaxpr/ppermute | solution.py:71
  3138.4 84.2 %all-reduce.9.cloned.1.call-start = ((), (), s32[]{:S(2)}) async-start(), calls=%async_computation.2 | async-start | bytes 524288 | tf_op jit(solution)/shard_map/while/body/eval_jaxpr/psum | solution.py:67
  3177.8 93.9 %collective-permute-start = (bf16[128,1024]{1,0:T(8,128)(2,1)S(1)}, bf16[128,1024]{1,0:T(8,128)(2,1)}, u32[]{:S(2)}, u32[]{:S(2)}) collective-permute-start(bf16[128,1024]{1,0:T(8,128)(2,1)S(1)} %get-tuple-element.903), channel_id=1, source_target_pairs={{0,1},{1,2},{2,3},{3,4},{4,5},{5,6},{6,7},{8,9},{9,10},{10,11},{11... | collective-permute-start | bytes 786440 | tf_op jit(solution)/shard_map/while/body/eval_jaxpr/ppermute | solution.py:71
  3318.8 84.2 %all-reduce.9.cloned.1.call-start = ((), (), s32[]{:S(2)}) async-start(), calls=%async_computation.2 | async-start | bytes 524288 | tf_op jit(solution)/shard_map/while/body/eval_jaxpr/psum | solution.py:67
  3358.1 93.9 %collective-permute-start = (bf16[128,1024]{1,0:T(8,128)(2,1)S(1)}, bf16[128,1024]{1,0:T(8,128)(2,1)}, u32[]{:S(2)}, u32[]{:S(2)}) collective-permute-start(bf16[128,1024]{1,0:T(8,128)(2,1)S(1)} %get-tuple-element.903), channel_id=1, source_target_pairs={{0,1},{1,2},{2,3},{3,4},{4,5},{5,6},{6,7},{8,9},{9,10},{10,11},{11... | collective-permute-start | bytes 786440 | tf_op jit(solution)/shard_map/while/body/eval_jaxpr/ppermute | solution.py:71
  3499.1 84.2 %all-reduce.9.cloned.1.call-start = ((), (), s32[]{:S(2)}) async-start(), calls=%async_computation.2 | async-start | bytes 524288 | tf_op jit(solution)/shard_map/while/body/eval_jaxpr/psum | solution.py:67
  3538.5 93.9 %collective-permute-start = (bf16[128,1024]{1,0:T(8,128)(2,1)S(1)}, bf16[128,1024]{1,0:T(8,128)(2,1)}, u32[]{:S(2)}, u32[]{:S(2)}) collective-permute-start(bf16[128,1024]{1,0:T(8,128)(2,1)S(1)} %get-tuple-element.903), channel_id=1, source_target_pairs={{0,1},{1,2},{2,3},{3,4},{4,5},{5,6},{6,7},{8,9},{9,10},{10,11},{11... | collective-permute-start | bytes 786440 | tf_op jit(solution)/shard_map/while/body/eval_jaxpr/ppermute | solution.py:71
  3679.5 84.2 %all-reduce.9.cloned.1.call-start = ((), (), s32[]{:S(2)}) async-start(), calls=%async_computation.2 | async-start | bytes 524288 | tf_op jit(solution)/shard_map/while/body/eval_jaxpr/psum | solution.py:67
  3718.8 93.9 %collective-permute-start = (bf16[128,1024]{1,0:T(8,128)(2,1)S(1)}, bf16[128,1024]{1,0:T(8,128)(2,1)}, u32[]{:S(2)}, u32[]{:S(2)}) collective-permute-start(bf16[128,1024]{1,0:T(8,128)(2,1)S(1)} %get-tuple-element.903), channel_id=1, source_target_pairs={{0,1},{1,2},{2,3},{3,4},{4,5},{5,6},{6,7},{8,9},{9,10},{10,11},{11... | collective-permute-start | bytes 786440 | tf_op jit(solution)/shard_map/while/body/eval_jaxpr/ppermute | solution.py:71
  3859.8 84.2 %all-reduce.9.cloned.1.call-start = ((), (), s32[]{:S(2)}) async-start(), calls=%async_computation.2 | async-start | bytes 524288 | tf_op jit(solution)/shard_map/while/body/eval_jaxpr/psum | solution.py:67
  3899.2 93.9 %collective-permute-start = (bf16[128,1024]{1,0:T(8,128)(2,1)S(1)}, bf16[128,1024]{1,0:T(8,128)(2,1)}, u32[]{:S(2)}, u32[]{:S(2)}) collective-permute-start(bf16[128,1024]{1,0:T(8,128)(2,1)S(1)} %get-tuple-element.903), channel_id=1, source_target_pairs={{0,1},{1,2},{2,3},{3,4},{4,5},{5,6},{6,7},{8,9},{9,10},{10,11},{11... | collective-permute-start | bytes 786440 | tf_op jit(solution)/shard_map/while/body/eval_jaxpr/ppermute | solution.py:71
  (217 other events, 4732.7 us)
Sparse Core Ops, SparseCore 0:
  28.6 39.2 all-reduce.4
  118.4 38.0 all-reduce.8
  208.9 39.0 all-reduce.4
  298.5 38.0 all-reduce.8
  390.3 37.9 all-reduce.4
  478.8 38.0 all-reduce.8
  570.6 37.9 all-reduce.4
  659.2 38.0 all-reduce.8
  751.0 37.9 all-reduce.4
  793.5 37.1 all-reduce.6
  839.5 38.0 all-reduce.8
  931.3 38.0 all-reduce.4
  1019.9 38.0 all-reduce.8
  1111.8 37.9 all-reduce.4
  1200.3 38.0 all-reduce.8
  1292.1 38.0 all-reduce.4
  1380.7 38.0 all-reduce.8
  1472.5 38.0 all-reduce.4
  1561.1 38.0 all-reduce.8
  1652.9 38.0 all-reduce.4
  1695.5 37.1 all-reduce.6
  1741.6 38.0 all-reduce.8
  1833.3 38.0 all-reduce.4
  1875.9 37.1 all-reduce.6
  1921.9 38.0 all-reduce.8
  2013.7 38.0 all-reduce.4
  2056.4 37.1 all-reduce.6
  2102.4 38.0 all-reduce.8
  2194.1 38.0 all-reduce.4
  2282.8 38.0 all-reduce.8
  2374.6 38.0 all-reduce.4
  2463.1 38.0 all-reduce.8
  2554.9 38.0 all-reduce.4
  2643.5 38.0 all-reduce.8
  2735.3 38.0 all-reduce.4
  2823.8 38.0 all-reduce.8
  2915.6 38.0 all-reduce.4
  3004.2 38.0 all-reduce.8
  3096.0 38.0 all-reduce.4
  3184.6 38.0 all-reduce.8
  3276.3 38.0 all-reduce.4
  3364.9 38.0 all-reduce.8
  3456.7 38.0 all-reduce.4
  3545.3 38.0 all-reduce.8
  3637.0 38.0 all-reduce.4
  3725.6 38.0 all-reduce.8
  3817.4 38.0 all-reduce.4
  3906.0 38.0 all-reduce.8
  (40 shorter events, 1483.8 us)
where the time goes:
time: 4040 us; the launch traced here: 4030 us
  waiting for transfers between devices  2960 us (73%)
  matrix products  760 us (19%)
  other arithmetic  166 us (4%)
  starting transfers between devices  78.5 us (2%)
    psum x44, waiting for transfers between devices, run_tick(): branch = lax.psum(part_out, 'tp')  1640 us
    psum x44, waiting for transfers between devices, run_tick(): spread = lax.psum(part_in, 'tp')  1310 us
    dot_general x44, matrix products, run_tick(): jnp.einsum('bd,bf->df', act_sv, gate_grad, preferred_element_type=jnp.flo...  223 us
    dot_general x44, matrix products, run_tick(): jnp.einsum('bf,bd->fd', post_sv, cur_grad, preferred_element_type=jnp.flo...  217 us
    dot_general x44, matrix products, run_tick(): jnp.einsum('bd,df->bf', cur_act, first_w[layer_idx], preferred_element_ty...  96.8 us
    dot_general x44, matrix products, run_tick(): jnp.einsum('bf,df->bd', gate_grad, first_w[layer_idx], preferred_element_...  91.8 us
  transfers between devices with their start and end apart: 132, of which 88 were waited for; matrix products, arithmetic and copies ran while one was open for 17% of the time, Pallas kernels for 0%

commit v1 on v0

v1 whole, which is shorter than its diff:
```python
import functools
import math

import jax
import jax.numpy as jnp
from jax import lax
from jax.experimental import pallas as pl
from jax.experimental.pallas import tpu as pltpu
from jax.sharding import PartitionSpec as P

F32 = jnp.float32
BF16 = jnp.bfloat16
CHUNK = 128
SPACING = 3
SHIFT = 0
GELU_C = math.sqrt(2.0 / math.pi)
GELU_K = 0.044715


def gelu_fwd(u):
    return 0.5 * u * (1.0 + jnp.tanh(GELU_C * (u + GELU_K * (u * u * u))))


def gelu_grad(u):
    sq = u * u
    th = jnp.tanh(GELU_C * (u + GELU_K * (sq * u)))
    return 0.5 * (1.0 + th) + (0.5 * GELU_C) * u * (1.0 - th * th) * (1.0 + (3.0 * GELU_K) * sq)


def dot(a, b):
    return jnp.dot(a, b, preferred_element_type=F32)


def dot_t(a, b):
    return lax.dot_general(a, b, (((1,), (1,)), ((), ())), preferred_element_type=F32)


def stack_kernel(n_pp, n_tp, rows_mb, spacing, shift, inv_count,
                 x_hbm, y_hbm, w1_hbm, w2_hbm,
                 a_out, dh_out, z_out, g_out, loss_out,
                 w1, w2, a_buf, dh_buf, u_buf, z_buf, g_buf, rs_recv, rs_send, hs_send,
                 own_part, t_buf, loss_acc, loss_all, loss_tot,
                 load_sem, rs_rsem, ag_rsem, rs_ssem, ag_ssem, out_sem,
                 lall_rsem, ltot_rsem, loss_ssem):
    t = lax.axis_index("tp")
    s = lax.axis_index("pp")
    last = n_pp - 1
    n_tok = a_buf.shape[2]
    ds = a_buf.shape[3]
    hidden = w1.shape[2]
    n_mb = n_tok // rows_mb
    n_layer = 2 * n_pp
    hc = 256

    def peer(d):
        return lax.rem(t + d, n_tp)

    far_first = (2, 1, 3)

    loads = []
    for layer in range(2):
        loads.append(pltpu.make_async_copy(w1_hbm.at[layer], w1.at[layer], load_sem.at[layer]))
        for j in range(n_tp):
            loads.append(pltpu.make_async_copy(
                w2_hbm.at[layer, :, pl.ds(j * ds, ds)], w2.at[layer, j], load_sem.at[2 + layer * n_tp + j]))
    x_loads = [pltpu.make_async_copy(x_hbm.at[:, pl.ds(j * ds, ds)], a_buf.at[0, j], load_sem.at[2 + 2 * n_tp + j])
               for j in range(n_tp)]
    y_load = pltpu.make_async_copy(y_hbm.at[:, pl.ds(pl.multiple_of(t * ds, ds), ds)], t_buf, load_sem.at[2 + 3 * n_tp])

    @pl.when(s == 0)
    def _():
        for c in x_loads:
            c.start()

    for c in loads:
        c.start()

    @pl.when(s == last)
    def _():
        y_load.start()
        loss_acc[...] = jnp.zeros_like(loss_acc)

    @pl.when(s == 0)
    def _():
        for c in x_loads:
            c.wait()

    for c in loads:
        c.wait()

    @pl.when(s == last)
    def _():
        y_load.wait()

    def rows_of(m):
        return pl.ds(pl.multiple_of(m * rows_mb, rows_mb), rows_mb)

    def wait_slices(buf, layer, lp, m, with_own):
        rows = rows_of(m)
        for d in ((0,) if with_own else ()) + (1, 3, 2):
            j = peer(d)
            ref = buf.at[layer, j, rows]
            pltpu.make_async_copy(ref, ref, ag_rsem.at[lp, j, m]).wait()

    def copy_out_slices(buf, out, layer, m, sem):
        rows = rows_of(m)
        for j in range(n_tp):
            pltpu.make_async_copy(buf.at[layer, j, rows], out.at[layer, rows, pl.ds(j * ds, ds)], sem).start()

    def send_part(lp, d, m):
        rows = rows_of(m)
        pltpu.make_async_remote_copy(
            src_ref=rs_send.at[lp, d - 1, rows], dst_ref=rs_recv.at[lp, d - 1, rows],
            send_sem=rs_ssem.at[lp], recv_sem=rs_rsem.at[lp, d - 1, m],
            device_id={"pp": s, "tp": peer(d)}, device_id_type=pl.DeviceIdType.MESH).start()

    def send_slice(lp, buf, layer, lp_dst, stage, d, m):
        rows = rows_of(m)
        pltpu.make_async_remote_copy(
            src_ref=hs_send.at[lp, rows], dst_ref=buf.at[layer, t, rows],
            send_sem=ag_ssem.at[lp], recv_sem=ag_rsem.at[lp_dst, t, m],
            device_id={"pp": stage, "tp": peer(d)}, device_id_type=pl.DeviceIdType.MESH).start()

    def partials(lp, m, fn):
        rows = rows_of(m)
        for d in far_first:
            rs_send[lp, d - 1, rows, :] = fn(peer(d)).astype(BF16)
            send_part(lp, d, m)
        own_part[lp] = fn(t)

    def reduce_own(lp, m):
        rows = rows_of(m)
        for d in (1, 3, 2):
            ref = rs_recv.at[lp, d - 1, rows]
            pltpu.make_async_copy(ref, ref, rs_rsem.at[lp, d - 1, m]).wait()
        acc = own_part[lp]
        for d in (1, 3, 2):
            acc = acc + rs_recv[lp, d - 1, rows, :].astype(F32)
        return acc

    def fwd_a(layer, m):
        rows = rows_of(m)
        if layer == 0:
            @pl.when(s > 0)
            def _():
                wait_slices(a_buf, 0, 0, m, True)
        else:
            wait_slices(a_buf, 1, 1, m, False)
        for c in range(hidden // hc):
            cols = slice(c * hc, (c + 1) * hc)
            acc = dot(a_buf[layer, 0, rows, :], w1[layer, 0:ds, cols])
            for j in range(1, n_tp):
                acc = acc + dot(a_buf[layer, j, rows, :], w1[layer, j * ds:(j + 1) * ds, cols])
            u = acc.astype(BF16)
            u_buf[layer, rows, cols] = u
            z_buf[layer, rows, cols] = gelu_fwd(u.astype(F32)).astype(BF16)
        partials(layer, m, lambda j: dot(z_buf[layer, rows, :], w2[layer, j]))
        copy_out_slices(a_buf, a_out, layer, m, out_sem.at[layer])
        pltpu.make_async_copy(z_buf.at[layer, rows], z_out.at[layer, rows], out_sem.at[4 + layer]).start()

    def fwd_b(layer, m):
        rows = rows_of(m)
        acc = reduce_own(layer, m)
        h = (a_buf[layer, t, rows, :].astype(F32) + acc).astype(BF16)
        if layer == 0:
            hs_send[0, rows, :] = h
            for d in far_first:
                send_slice(0, a_buf, 1, 1, s, d, m)
            a_buf[1, t, rows, :] = h
        else:
            @pl.when(s < last)
            def _():
                hs_send[1, rows, :] = h
                for d in far_first + (0,):
                    send_slice(1, a_buf, 0, 0, s + 1, d, m)

            @pl.when(s == last)
            def _():
                err = h.astype(F32) - t_buf[rows, :].astype(F32)
                grad = (err * inv_count).astype(BF16)
                hs_send[1, rows, :] = grad
                for d in far_first:
                    send_slice(1, dh_buf, 1, 3, s, d, m)
                dh_buf[1, t, rows, :] = grad
                half = 0.5 * err * err
                half = jnp.sum(half.reshape(rows_mb // 8, 8, ds), axis=0)
                part = half[:, :128]
                for q in range(1, ds // 128):
                    part = part + half[:, q * 128:(q + 1) * 128]
                loss_acc[...] = loss_acc[...] + part

                @pl.when(m == n_mb - 1)
                def _():
                    loss_all[t] = loss_acc[...]
                    for d in far_first:
                        pltpu.make_async_remote_copy(
                            src_ref=loss_acc, dst_ref=loss_all.at[t],
                            send_sem=loss_ssem.at[0], recv_sem=lall_rsem.at[t],
                            device_id={"pp": s, "tp": peer(d)}, device_id_type=pl.DeviceIdType.MESH).start()

    def pass_loss():
        @pl.when(s == last)
        def _():
            for d in (1, 3, 2):
                j = peer(d)
                pltpu.make_async_copy(loss_all.at[j], loss_all.at[j], lall_rsem.at[j]).wait()
            tot = loss_all[0]
            for j in range(1, n_tp):
                tot = tot + loss_all[j]
            loss_tot[...] = tot

        @pl.when(s < last)
        def _():
            pltpu.make_async_copy(loss_tot, loss_tot, ltot_rsem).wait()

        @pl.when(s > 0)
        def _():
            pltpu.make_async_remote_copy(
                src_ref=loss_tot, dst_ref=loss_tot, send_sem=loss_ssem.at[1], recv_sem=ltot_rsem,
                device_id={"pp": s - 1, "tp": t}, device_id_type=pl.DeviceIdType.MESH).start()

    def bwd_a(layer, m):
        lp = 2 + layer
        rows = rows_of(m)
        if layer == 1:
            @pl.when(s < last)
            def _():
                wait_slices(dh_buf, 1, 3, m, True)

            @pl.when(s == last)
            def _():
                wait_slices(dh_buf, 1, 3, m, False)
        else:
            wait_slices(dh_buf, 0, 2, m, False)
        for c in range(hidden // hc):
            cols = slice(c * hc, (c + 1) * hc)
            acc = dot_t(dh_buf[layer, 0, rows, :], w2[layer, 0, cols, :])
            for j in range(1, n_tp):
                acc = acc + dot_t(dh_buf[layer, j, rows, :], w2[layer, j, cols, :])
            u = u_buf[layer, rows, cols].astype(F32)
            g_buf[layer, rows, cols] = (gelu_grad(u) * acc).astype(BF16)

        def send():
            partials(lp, m, lambda j: dot_t(
                g_buf[layer, rows, :], w1[layer, pl.ds(pl.multiple_of(j * ds, ds), ds), :]))

        if layer == 1:
            send()
        else:
            pl.when(s > 0)(send)
        copy_out_slices(dh_buf, dh_out, layer, m, out_sem.at[2 + layer])
        pltpu.make_async_copy(g_buf.at[layer, rows], g_out.at[layer, rows], out_sem.at[6 + layer]).start()
        if layer == 1:
            pl.when(m == n_mb - 1)(pass_loss)

    def bwd_b(layer, m):
        lp = 2 + layer
        rows = rows_of(m)
        acc = reduce_own(lp, m)
        h = (dh_buf[layer, t, rows, :].astype(F32) + acc).astype(BF16)
        hs_send[lp, rows, :] = h
        if layer == 1:
            for d in far_first:
                send_slice(lp, dh_buf, 0, 2, s, d, m)
            dh_buf[0, t, rows, :] = h
        else:
            for d in far_first + (0,):
                send_slice(lp, dh_buf, 1, 3, s - 1, d, m)

    def at_tick(k, start, fn, layer, extra=None):
        q = k - start
        m = lax.div(q, spacing)
        ok = (q >= 0) & (lax.rem(q, spacing) == 0) & (m < n_mb)
        if extra is not None:
            ok = ok & extra
        pl.when(ok)(lambda: fn(layer, m))

    f_start = 4 * s
    b_start = 2 * n_layer + shift + 4 * (last - s)

    def tick(k, carry):
        at_tick(k, f_start + 1, fwd_b, 0)
        at_tick(k, f_start + 3, fwd_b, 1)
        at_tick(k, b_start + 1, bwd_b, 1)
        at_tick(k, b_start + 3, bwd_b, 0, s > 0)
        at_tick(k, b_start, bwd_a, 1)
        at_tick(k, b_start + 2, bwd_a, 0)
        at_tick(k, f_start, fwd_a, 0)
        at_tick(k, f_start + 2, fwd_a, 1)
        return carry

    n_ticks = 4 * n_layer + shift + spacing * (n_mb - 1)
    lax.fori_loop(0, n_ticks, tick, 0)

    for layer in range(2):
        for i in range(4):
            pltpu.make_async_copy(z_buf.at[layer], z_out.at[layer], out_sem.at[2 * i + layer]).wait()

    def wait_three(sem):
        pltpu.make_async_copy(rs_send.at[0], rs_send.at[0], sem).wait()

    def wait_four(sem):
        pltpu.make_async_copy(a_buf.at[0], a_buf.at[0], sem).wait()

    for lp in (0, 1, 3):
        wait_three(rs_ssem.at[lp])
    wait_three(ag_ssem.at[0])
    wait_three(ag_ssem.at[3])

    @pl.when(s < last)
    def _():
        wait_four(ag_ssem.at[1])

    @pl.when(s == last)
    def _():
        wait_three(ag_ssem.at[1])
        pltpu.make_async_copy(loss_all.at[0:3], loss_all.at[0:3], loss_ssem.at[0]).wait()

    @pl.when(s > 0)
    def _():
        wait_three(rs_ssem.at[2])
        wait_four(ag_ssem.at[2])
        pltpu.make_async_copy(loss_tot, loss_tot, loss_ssem.at[1]).wait()

    loss_out[...] = loss_tot[...]


def solution(mesh):
    n_pp = mesh.shape["pp"]
    n_tp = mesh.shape["tp"]

    def device_program(x_loc, y_loc, w_in, w_out):
        n_tok = x_loc.shape[0] * x_loc.shape[1]
        d_model = x_loc.shape[2]
        hidden = w_in.shape[3]
        ds = d_model // n_tp
        rows_mb = CHUNK
        n_mb = n_tok // rows_mb
        inv_count = 1.0 / (n_tok * d_model)
        kernel = functools.partial(stack_kernel, n_pp, n_tp, rows_mb, SPACING, SHIFT, inv_count)
        any_spec = pl.BlockSpec(memory_space=pl.ANY)
        dma = pltpu.SemaphoreType.DMA
        a, dh, z, g, loss = pl.pallas_call(
            kernel,
            out_shape=[
                jax.ShapeDtypeStruct((2, n_tok, d_model), BF16),
                jax.ShapeDtypeStruct((2, n_tok, d_model), BF16),
                jax.ShapeDtypeStruct((2, n_tok, hidden), BF16),
                jax.ShapeDtypeStruct((2, n_tok, hidden), BF16),
                jax.ShapeDtypeStruct((8, 128), F32),
            ],
            in_specs=[any_spec] * 4,
            out_specs=[any_spec] * 4 + [pl.BlockSpec(memory_space=pltpu.VMEM)],
            scratch_shapes=[
                pltpu.VMEM((2, d_model, hidden), BF16),
                pltpu.VMEM((2, n_tp, hidden, ds), BF16),
                pltpu.VMEM((2, n_tp, n_tok, ds), BF16),
                pltpu.VMEM((2, n_tp, n_tok, ds), BF16),
                pltpu.VMEM((2, n_tok, hidden), BF16),
                pltpu.VMEM((2, n_tok, hidden), BF16),
                pltpu.VMEM((2, n_tok, hidden), BF16),
                pltpu.VMEM((4, 3, n_tok, ds), BF16),
                pltpu.VMEM((4, 3, n_tok, ds), BF16),
                pltpu.VMEM((4, n_tok, ds), BF16),
                pltpu.VMEM((4, rows_mb, ds), F32),
                pltpu.VMEM((n_tok, ds), BF16),
                pltpu.VMEM((8, 128), F32),
                pltpu.VMEM((n_tp, 8, 128), F32),
                pltpu.VMEM((8, 128), F32),
                dma((3 + 3 * n_tp,)),
                dma((4, 3, n_mb)),
                dma((4, n_tp, n_mb)),
                dma((4,)),
                dma((4,)),
                dma((8,)),
                dma((n_tp,)),
                dma,
                dma((2,)),
            ],
            compiler_params=pltpu.CompilerParams(has_side_effects=True, vmem_limit_bytes=60 * 1024 * 1024),
            cost_estimate=pl.CostEstimate(flops=10**11, bytes_accessed=10**8, transcendentals=0),
            name="mlp_stack",
        )(x_loc.reshape(n_tok, d_model), y_loc.reshape(n_tok, d_model), w_in[0], w_out[0])
        grad_first = jnp.einsum("ltd,ltf->ldf", a, g, preferred_element_type=F32)[None]
        grad_second = jnp.einsum("ltf,ltd->lfd", z, dh, preferred_element_type=F32)[None]
        loss_val = (jnp.sum(loss) * inv_count).reshape(1)
        return grad_first, grad_second, loss_val

    return jax.shard_map(
        device_program,
        mesh=mesh,
        in_specs=(P("dp", None, None), P("dp", None, None), P("pp", None, None, "tp"), P("pp", None, "tp", None)),
        out_specs=(P(("dp", "pp"), None, None, "tp"), P(("dp", "pp"), None, "tp", None), P("dp")),
        check_vma=False,
    )
```

time: 4040 us -> 552 us (0.14)
  waiting for transfers between devices: 2960 us -> 0 us
  matrix products: 760 us -> 18.4 us
  Pallas kernels: 0 us -> 530 us
  other arithmetic: 166 us -> 1.29 us
  starting transfers between devices: 78.5 us -> 0 us
    psum x88 -> x0, waiting for transfers between devices: 2960 us -> none  [the longest x44 1640 us: run_tick(): branch = lax.psum(part_out, 'tp')]
    dot_general x264 -> x2, matrix products: 760 us -> 18.4 us  [the longest x1 11.6 us: device_program(): jnp.einsum('ltd,ltf->ldf', a, g, preferred_element_type=F32)[None]]
    pallas_call x0 -> x1, Pallas kernels: none -> 530 us  [device_program(): pl.pallas_call(kernel, out_shape=[jax.ShapeDtypeStruct((2, n_tok, d_model...]
    ppermute x44 -> x0, starting transfers between devices: 73 us -> none  [the longest x22 44.2 us: run_tick(): recv_act = lax.ppermute(cur_act, 'pp', fwd_pairs)]
    dynamic_update_slice x44 -> x0, other arithmetic: 59.1 us -> none  [run_tick(): lax.dynamic_update_index_in_dim(store_in[layer_idx], cur_act, slot_fwd, 0)]
    reduce_sum x22 -> x1, other arithmetic: 44.3 us -> 1.29 us  [device_program(): loss_val = (jnp.sum(loss) * inv_count).reshape(1)]
  transfers between devices with their start and end apart: 132 -> 0, of which waited for: 88 -> 0; matrix products, arithmetic and copies ran while one was open for 17% -> 0% of each run, Pallas kernels for 0% -> 0%
where the time goes in v1:
time: 552 us
  Pallas kernels  530 us (96%)
  matrix products  18.4 us (3%)
    pallas_call x1, Pallas kernels, device_program(): pl.pallas_call(kernel, out_shape=[jax.ShapeDtypeStruct((2, n_tok, d_model...  530 us
    dot_general x1, matrix products, device_program(): jnp.einsum('ltd,ltf->ldf', a, g, preferred_element_type=F32)[None]  11.6 us

profile of v1, /device:TPU:96, one launch (start us, length us, event | category | flops | bytes accessed | tf_op | source)
XLA Modules:
  0.0 552.0 jit_solution(6521662949651755296)
XLA Ops:
  0.6 529.9 %mlp_stack.1 = (bf16[2,1024,1024]{2,1,0:T(8,128)(2,1)}, bf16[2,1024,1024]{2,1,0:T(8,128)(2,1)}, bf16[2,1024,1024]{2,1,0:T(8,128)(2,1)}, bf16[2,1024,1024]{2,1,0:T(8,128)(2,1)}, f32[8,128]{1,0:T(8,128)}) custom-call(bf16[1024,1024]{1,0:T(8,128)(2,1)} %bitcast.15, bf16[1024,1024]{1,0:T(8,128)(2,1)} %bitcast.16, bf16[2,1024,1024]{2,1,0:T(8,128)(2,1)} %bitcast.13, ...), custom_call_target="tpu_custom_call" | custom-call | flops 99999997952 | bytes 100000000 | tf_op jit(solution)/shard_map/mlp_stack/pallas_call | solution.py:343
  530.5 1.3 reduce_sum.9
  532.4 0.0 copy-start
  532.4 0.0 copy-start.1
  532.5 11.6 %convolution_bitcast_fusion.1 = f32[1,2,1024,1024]{3,2,1,0:T(8,128)} fusion(bf16[2,1024,1024]{2,1,0:T(8,128)(2,1)} %get-tuple-element.8, bf16[2,1024,1024]{2,1,0:T(8,128)(2,1)} %get-tuple-element.9), kind=kOutput, calls=%fused_computation.1 | convolution fusion | flops 4294967296 | bytes 16777216 | tf_op jit(solution)/shard_map/ltd,ltf->ldf/dot_general | solution.py:384
  544.0 0.0 copy-done
  544.0 0.0 copy-done.1
  544.0 6.8 %convolution_bitcast_fusion = f32[1,2,1024,1024]{3,2,1,0:T(8,128)} fusion(bf16[2,1024,1024]{2,1,0:T(8,128)(2,1)S(1)} %copy-done.1, bf16[2,1024,1024]{2,1,0:T(8,128)(2,1)S(1)} %copy-done), kind=kOutput, calls=%fused_computation | convolution fusion | flops 4294967296 | bytes 16777216 | tf_op jit(solution)/shard_map/ltf,ltd->lfd/dot_general | solution.py:385
Async XLA Ops:
  532.4 11.6 %copy-start = (bf16[2,1024,1024]{2,1,0:T(8,128)(2,1)S(1)}, bf16[2,1024,1024]{2,1,0:T(8,128)(2,1)}, u32[]{:S(2)}) copy-start(bf16[2,1024,1024]{2,1,0:T(8,128)(2,1)} %get-tuple-element.11) | copy-start | bytes 12582916
  532.4 11.6 %copy-start.1 = (bf16[2,1024,1024]{2,1,0:T(8,128)(2,1)S(1)}, bf16[2,1024,1024]{2,1,0:T(8,128)(2,1)}, u32[]{:S(2)}) copy-start(bf16[2,1024,1024]{2,1,0:T(8,128)(2,1)} %get-tuple-element.10) | copy-start | bytes 12582916

commit v2 on v1

--- a/solution.py
+++ b/solution.py
@@ -10,8 +10,8 @@
 
 F32 = jnp.float32
 BF16 = jnp.bfloat16
-CHUNK = 128
-SPACING = 3
+CHUNK = 64
+SPACING = 1
 SHIFT = 0
 GELU_C = math.sqrt(2.0 / math.pi)
 GELU_K = 0.044715
@@ -267,26 +267,35 @@
             for d in far_first + (0,):
                 send_slice(lp, dh_buf, 1, 3, s - 1, d, m)
 
-    def at_tick(k, start, fn, layer, extra=None):
-        q = k - start
-        m = lax.div(q, spacing)
-        ok = (q >= 0) & (lax.rem(q, spacing) == 0) & (m < n_mb)
-        if extra is not None:
-            ok = ok & extra
-        pl.when(ok)(lambda: fn(layer, m))
-
     f_start = 4 * s
     b_start = 2 * n_layer + shift + 4 * (last - s)
 
     def tick(k, carry):
-        at_tick(k, f_start + 1, fwd_b, 0)
-        at_tick(k, f_start + 3, fwd_b, 1)
-        at_tick(k, b_start + 1, bwd_b, 1)
-        at_tick(k, b_start + 3, bwd_b, 0, s > 0)
-        at_tick(k, b_start, bwd_a, 1)
-        at_tick(k, b_start + 2, bwd_a, 0)
-        at_tick(k, f_start, fwd_a, 0)
-        at_tick(k, f_start + 2, fwd_a, 1)
+        bias = 8 * n_pp + 2 * n_layer + shift + 4
+        bias = spacing * (-(-bias // spacing))
+        turn = {}
+        for name, start in (("f", f_start), ("b", b_start)):
+            q = k - start + bias
+            turn[name] = (lax.div(q, spacing) - bias // spacing, lax.rem(q, spacing) if spacing > 1 else None)
+
+        def at(name, offset, fn, layer, extra=None):
+            m, phase = turn[name]
+            m = m - offset // spacing
+            ok = (m >= 0) & (m < n_mb)
+            if phase is not None:
+                ok = ok & (phase == offset % spacing)
+            if extra is not None:
+                ok = ok & extra
+            pl.when(ok)(lambda: fn(layer, m))
+
+        at("b", 3, bwd_b, 0, s > 0)
+        at("b", 2, bwd_a, 0)
+        at("b", 1, bwd_b, 1)
+        at("b", 0, bwd_a, 1)
+        at("f", 3, fwd_b, 1)
+        at("f", 2, fwd_a, 1)
+        at("f", 1, fwd_b, 0)
+        at("f", 0, fwd_a, 0)
         return carry
 
     n_ticks = 4 * n_layer + shift + spacing * (n_mb - 1)

time: 552 us -> 482 us (0.87)
  Pallas kernels: 530 us -> 460 us
    pallas_call x1, Pallas kernels: 530 us -> 460 us  [device_program(): pl.pallas_call(kernel, out_shape=[jax.ShapeDtypeStruct((2, n_tok, d_model...]
where the time goes in v2:
time: 482 us
  Pallas kernels  460 us (95%)
  matrix products  18.4 us (4%)
    pallas_call x1, Pallas kernels, device_program(): pl.pallas_call(kernel, out_shape=[jax.ShapeDtypeStruct((2, n_tok, d_model...  460 us
    dot_general x1, matrix products, device_program(): jnp.einsum('ltd,ltf->ldf', a, g, preferred_element_type=F32)[None]  11.6 us

profile of v2, /device:TPU:96, one launch (start us, length us, event | category | flops | bytes accessed | tf_op | source)
XLA Modules:
  0.0 482.1 jit_solution(10738028826177169029)
XLA Ops:
  0.6 460.0 %mlp_stack.1 = (bf16[2,1024,1024]{2,1,0:T(8,128)(2,1)}, bf16[2,1024,1024]{2,1,0:T(8,128)(2,1)}, bf16[2,1024,1024]{2,1,0:T(8,128)(2,1)}, bf16[2,1024,1024]{2,1,0:T(8,128)(2,1)}, f32[8,128]{1,0:T(8,128)}) custom-call(bf16[1024,1024]{1,0:T(8,128)(2,1)} %bitcast.15, bf16[1024,1024]{1,0:T(8,128)(2,1)} %bitcast.16, bf16[2,1024,1024]{2,1,0:T(8,128)(2,1)} %bitcast.13, ...), custom_call_target="tpu_custom_call" | custom-call | flops 99999997952 | bytes 100000000 | tf_op jit(solution)/shard_map/mlp_stack/pallas_call | solution.py:352
  460.6 1.3 reduce_sum.9
  462.5 0.0 copy-start
  462.6 0.0 copy-start.1
  462.6 11.6 %convolution_bitcast_fusion.1 = f32[1,2,1024,1024]{3,2,1,0:T(8,128)} fusion(bf16[2,1024,1024]{2,1,0:T(8,128)(2,1)} %get-tuple-element.8, bf16[2,1024,1024]{2,1,0:T(8,128)(2,1)} %get-tuple-element.9), kind=kOutput, calls=%fused_computation.1 | convolution fusion | flops 4294967296 | bytes 16777216 | tf_op jit(solution)/shard_map/ltd,ltf->ldf/dot_general | solution.py:393
  474.1 0.0 copy-done
  474.1 0.0 copy-done.1
  474.1 6.8 %convolution_bitcast_fusion = f32[1,2,1024,1024]{3,2,1,0:T(8,128)} fusion(bf16[2,1024,1024]{2,1,0:T(8,128)(2,1)S(1)} %copy-done.1, bf16[2,1024,1024]{2,1,0:T(8,128)(2,1)S(1)} %copy-done), kind=kOutput, calls=%fused_computation | convolution fusion | flops 4294967296 | bytes 16777216 | tf_op jit(solution)/shard_map/ltf,ltd->lfd/dot_general | solution.py:394
Async XLA Ops:
  462.5 11.6 %copy-start = (bf16[2,1024,1024]{2,1,0:T(8,128)(2,1)S(1)}, bf16[2,1024,1024]{2,1,0:T(8,128)(2,1)}, u32[]{:S(2)}) copy-start(bf16[2,1024,1024]{2,1,0:T(8,128)(2,1)} %get-tuple-element.11) | copy-start | bytes 12582916
  462.6 11.6 %copy-start.1 = (bf16[2,1024,1024]{2,1,0:T(8,128)(2,1)S(1)}, bf16[2,1024,1024]{2,1,0:T(8,128)(2,1)}, u32[]{:S(2)}) copy-start(bf16[2,1024,1024]{2,1,0:T(8,128)(2,1)} %get-tuple-element.10) | copy-start | bytes 12582916

commit v3 on v2

--- a/solution.py
+++ b/solution.py
@@ -12,6 +12,8 @@
 BF16 = jnp.bfloat16
 CHUNK = 64
 SPACING = 1
+HOST = 1
+GRAD_TILE = 512
 SHIFT = 0
 GELU_C = math.sqrt(2.0 / math.pi)
 GELU_K = 0.044715
@@ -40,11 +42,15 @@
                  a_out, dh_out, z_out, g_out, loss_out,
                  w1, w2, a_buf, dh_buf, u_buf, z_buf, g_buf, rs_recv, rs_send, hs_send,
                  own_part, t_buf, loss_acc, loss_all, loss_tot,
+                 guest_recv, guest_own, own_send, guest_send,
                  load_sem, rs_rsem, ag_rsem, rs_ssem, ag_ssem, out_sem,
+                 guest_rsem, guest_ssem, own_ssem,
                  lall_rsem, ltot_rsem, loss_ssem):
     t = lax.axis_index("tp")
     s = lax.axis_index("pp")
     last = n_pp - 1
+    away = last
+    host_stage = HOST
     n_tok = a_buf.shape[2]
     ds = a_buf.shape[3]
     hidden = w1.shape[2]
@@ -57,11 +63,11 @@
 
     far_first = (2, 1, 3)
 
-    loads = []
+    loads = [[], []]
     for layer in range(2):
-        loads.append(pltpu.make_async_copy(w1_hbm.at[layer], w1.at[layer], load_sem.at[layer]))
+        loads[layer].append(pltpu.make_async_copy(w1_hbm.at[layer], w1.at[layer], load_sem.at[layer]))
         for j in range(n_tp):
-            loads.append(pltpu.make_async_copy(
+            loads[layer].append(pltpu.make_async_copy(
                 w2_hbm.at[layer, :, pl.ds(j * ds, ds)], w2.at[layer, j], load_sem.at[2 + layer * n_tp + j]))
     x_loads = [pltpu.make_async_copy(x_hbm.at[:, pl.ds(j * ds, ds)], a_buf.at[0, j], load_sem.at[2 + 2 * n_tp + j])
                for j in range(n_tp)]
@@ -72,10 +78,10 @@
         for c in x_loads:
             c.start()
 
-    for c in loads:
+    for c in loads[0] + loads[1]:
         c.start()
 
-    @pl.when(s == last)
+    @pl.when(s == host_stage)
     def _():
         y_load.start()
         loss_acc[...] = jnp.zeros_like(loss_acc)
@@ -85,10 +91,10 @@
         for c in x_loads:
             c.wait()
 
-    for c in loads:
+    for c in loads[0]:
         c.wait()
 
-    @pl.when(s == last)
+    @pl.when(s == host_stage)
     def _():
         y_load.wait()
 
@@ -109,10 +115,20 @@
 
     def send_part(lp, d, m):
         rows = rows_of(m)
-        pltpu.make_async_remote_copy(
-            src_ref=rs_send.at[lp, d - 1, rows], dst_ref=rs_recv.at[lp, d - 1, rows],
-            send_sem=rs_ssem.at[lp], recv_sem=rs_rsem.at[lp, d - 1, m],
-            device_id={"pp": s, "tp": peer(d)}, device_id_type=pl.DeviceIdType.MESH).start()
+
+        @pl.when(s < away)
+        def _():
+            pltpu.make_async_remote_copy(
+                src_ref=rs_send.at[lp, d - 1, rows], dst_ref=rs_recv.at[lp, d - 1, rows],
+                send_sem=rs_ssem.at[lp], recv_sem=rs_rsem.at[lp, d - 1, m],
+                device_id={"pp": s, "tp": peer(d)}, device_id_type=pl.DeviceIdType.MESH).start()
+
+        @pl.when(s >= away)
+        def _():
+            pltpu.make_async_remote_copy(
+                src_ref=rs_send.at[lp, d - 1, rows], dst_ref=guest_recv.at[lp, d - 1, rows],
+                send_sem=rs_ssem.at[lp], recv_sem=guest_rsem.at[lp, d - 1, m],
+                device_id={"pp": host_stage, "tp": peer(d)}, device_id_type=pl.DeviceIdType.MESH).start()
 
     def send_slice(lp, buf, layer, lp_dst, stage, d, m):
         rows = rows_of(m)
@@ -121,12 +137,32 @@
             send_sem=ag_ssem.at[lp], recv_sem=ag_rsem.at[lp_dst, t, m],
             device_id={"pp": stage, "tp": peer(d)}, device_id_type=pl.DeviceIdType.MESH).start()
 
-    def partials(lp, m, fn):
+    def send_guest(lp, buf, layer, lp_dst, stage, m):
+        rows = rows_of(m)
+        for d in far_first + (0,):
+            pltpu.make_async_remote_copy(
+                src_ref=guest_send.at[lp, rows], dst_ref=buf.at[layer, t, rows],
+                send_sem=guest_ssem.at[lp], recv_sem=ag_rsem.at[lp_dst, t, m],
+                device_id={"pp": stage, "tp": peer(d)}, device_id_type=pl.DeviceIdType.MESH).start()
+
+    def partials(lp, m, buf, layer, fn):
         rows = rows_of(m)
         for d in far_first:
             rs_send[lp, d - 1, rows, :] = fn(peer(d)).astype(BF16)
             send_part(lp, d, m)
-        own_part[lp] = fn(t)
+        own = buf[layer, t, rows, :].astype(F32) + fn(t)
+
+        @pl.when(s < away)
+        def _():
+            own_part[lp] = own
+
+        @pl.when(s >= away)
+        def _():
+            own_send[lp, rows, :] = own
+            pltpu.make_async_remote_copy(
+                src_ref=own_send.at[lp, rows], dst_ref=guest_own.at[lp, rows],
+                send_sem=own_ssem.at[lp], recv_sem=guest_rsem.at[lp, 3, m],
+                device_id={"pp": host_stage, "tp": t}, device_id_type=pl.DeviceIdType.MESH).start()
 
     def reduce_own(lp, m):
         rows = rows_of(m)
@@ -136,7 +172,19 @@
         acc = own_part[lp]
         for d in (1, 3, 2):
             acc = acc + rs_recv[lp, d - 1, rows, :].astype(F32)
-        return acc
+        return acc.astype(BF16)
+
+    def reduce_guest(lp, m):
+        rows = rows_of(m)
+        for d in (1, 3, 2):
+            ref = guest_recv.at[lp, d - 1, rows]
+            pltpu.make_async_copy(ref, ref, guest_rsem.at[lp, d - 1, m]).wait()
+        ref = guest_own.at[lp, rows]
+        pltpu.make_async_copy(ref, ref, guest_rsem.at[lp, 3, m]).wait()
+        acc = guest_own[lp, rows, :]
+        for d in (1, 3, 2):
+            acc = acc + guest_recv[lp, d - 1, rows, :].astype(F32)
+        return acc.astype(BF16)
 
     def fwd_a(layer, m):
         rows = rows_of(m)
@@ -145,7 +193,13 @@
             def _():
                 wait_slices(a_buf, 0, 0, m, True)
         else:
-            wait_slices(a_buf, 1, 1, m, False)
+            @pl.when(s < away)
+            def _():
+                wait_slices(a_buf, 1, 1, m, False)
+
+            @pl.when(s >= away)
+            def _():
+                wait_slices(a_buf, 1, 1, m, True)
         for c in range(hidden // hc):
             cols = slice(c * hc, (c + 1) * hc)
             acc = dot(a_buf[layer, 0, rows, :], w1[layer, 0:ds, cols])
@@ -154,55 +208,51 @@
             u = acc.astype(BF16)
             u_buf[layer, rows, cols] = u
             z_buf[layer, rows, cols] = gelu_fwd(u.astype(F32)).astype(BF16)
-        partials(layer, m, lambda j: dot(z_buf[layer, rows, :], w2[layer, j]))
+        partials(layer, m, a_buf, layer, lambda j: dot(z_buf[layer, rows, :], w2[layer, j]))
         copy_out_slices(a_buf, a_out, layer, m, out_sem.at[layer])
         pltpu.make_async_copy(z_buf.at[layer, rows], z_out.at[layer, rows], out_sem.at[4 + layer]).start()
 
     def fwd_b(layer, m):
         rows = rows_of(m)
-        acc = reduce_own(layer, m)
-        h = (a_buf[layer, t, rows, :].astype(F32) + acc).astype(BF16)
+        h = reduce_own(layer, m)
+        hs_send[layer, rows, :] = h
         if layer == 0:
-            hs_send[0, rows, :] = h
             for d in far_first:
                 send_slice(0, a_buf, 1, 1, s, d, m)
             a_buf[1, t, rows, :] = h
         else:
-            @pl.when(s < last)
-            def _():
-                hs_send[1, rows, :] = h
-                for d in far_first + (0,):
-                    send_slice(1, a_buf, 0, 0, s + 1, d, m)
-
-            @pl.when(s == last)
-            def _():
-                err = h.astype(F32) - t_buf[rows, :].astype(F32)
-                grad = (err * inv_count).astype(BF16)
-                hs_send[1, rows, :] = grad
-                for d in far_first:
-                    send_slice(1, dh_buf, 1, 3, s, d, m)
-                dh_buf[1, t, rows, :] = grad
-                half = 0.5 * err * err
-                half = jnp.sum(half.reshape(rows_mb // 8, 8, ds), axis=0)
-                part = half[:, :128]
-                for q in range(1, ds // 128):
-                    part = part + half[:, q * 128:(q + 1) * 128]
-                loss_acc[...] = loss_acc[...] + part
-
-                @pl.when(m == n_mb - 1)
-                def _():
-                    loss_all[t] = loss_acc[...]
-                    for d in far_first:
-                        pltpu.make_async_remote_copy(
-                            src_ref=loss_acc, dst_ref=loss_all.at[t],
-                            send_sem=loss_ssem.at[0], recv_sem=lall_rsem.at[t],
-                            device_id={"pp": s, "tp": peer(d)}, device_id_type=pl.DeviceIdType.MESH).start()
+            for d in far_first + (0,):
+                send_slice(1, a_buf, 0, 0, s + 1, d, m)
+
+    def fwd_b_guest(layer, m):
+        rows = rows_of(m)
+        h = reduce_guest(layer, m)
+        if layer == 0:
+            guest_send[0, rows, :] = h
+            send_guest(0, a_buf, 1, 1, last, m)
+            return
+        err = h.astype(F32) - t_buf[rows, :].astype(F32)
+        guest_send[1, rows, :] = (err * inv_count).astype(BF16)
+        send_guest(1, dh_buf, 1, 3, last, m)
+        half = 0.5 * err * err
+        half = jnp.sum(half.reshape(rows_mb // 8, 8, ds), axis=0)
+        part = half[:, :128]
+        for q in range(1, ds // 128):
+            part = part + half[:, q * 128:(q + 1) * 128]
+        loss_acc[...] = loss_acc[...] + part
+
+        @pl.when(m == n_mb - 1)
+        def _():
+            for d in far_first + (0,):
+                pltpu.make_async_remote_copy(
+                    src_ref=loss_acc, dst_ref=loss_all.at[t],
+                    send_sem=loss_ssem.at[0], recv_sem=lall_rsem.at[t],
+                    device_id={"pp": last, "tp": peer(d)}, device_id_type=pl.DeviceIdType.MESH).start()
 
     def pass_loss():
         @pl.when(s == last)
         def _():
-            for d in (1, 3, 2):
-                j = peer(d)
+            for j in range(n_tp):
                 pltpu.make_async_copy(loss_all.at[j], loss_all.at[j], lall_rsem.at[j]).wait()
             tot = loss_all[0]
             for j in range(1, n_tp):
@@ -223,15 +273,15 @@
         lp = 2 + layer
         rows = rows_of(m)
         if layer == 1:
-            @pl.when(s < last)
+            wait_slices(dh_buf, 1, 3, m, True)
+        else:
+            @pl.when(s < away)
             def _():
-                wait_slices(dh_buf, 1, 3, m, True)
-
-            @pl.when(s == last)
+                wait_slices(dh_buf, 0, 2, m, False)
+
+            @pl.when(s >= away)
             def _():
-                wait_slices(dh_buf, 1, 3, m, False)
-        else:
-            wait_slices(dh_buf, 0, 2, m, False)
+                wait_slices(dh_buf, 0, 2, m, True)
         for c in range(hidden // hc):
             cols = slice(c * hc, (c + 1) * hc)
             acc = dot_t(dh_buf[layer, 0, rows, :], w2[layer, 0, cols, :])
@@ -241,7 +291,7 @@
             g_buf[layer, rows, cols] = (gelu_grad(u) * acc).astype(BF16)
 
         def send():
-            partials(lp, m, lambda j: dot_t(
+            partials(lp, m, dh_buf, layer, lambda j: dot_t(
                 g_buf[layer, rows, :], w1[layer, pl.ds(pl.multiple_of(j * ds, ds), ds), :]))
 
         if layer == 1:
@@ -256,8 +306,7 @@
     def bwd_b(layer, m):
         lp = 2 + layer
         rows = rows_of(m)
-        acc = reduce_own(lp, m)
-        h = (dh_buf[layer, t, rows, :].astype(F32) + acc).astype(BF16)
+        h = reduce_own(lp, m)
         hs_send[lp, rows, :] = h
         if layer == 1:
             for d in far_first:
@@ -267,11 +316,25 @@
             for d in far_first + (0,):
                 send_slice(lp, dh_buf, 1, 3, s - 1, d, m)
 
+    def bwd_b_guest(layer, m):
+        lp = 2 + layer
+        rows = rows_of(m)
+        guest_send[lp, rows, :] = reduce_guest(lp, m)
+        if layer == 1:
+            send_guest(lp, dh_buf, 0, 2, last, m)
+        else:
+            send_guest(lp, dh_buf, 1, 3, last - 1, m)
+
     f_start = 4 * s
     b_start = 2 * n_layer + shift + 4 * (last - s)
 
     def tick(k, carry):
-        bias = 8 * n_pp + 2 * n_layer + shift + 4
+        @pl.when(k == 1)
+        def _():
+            for c in loads[1]:
+                c.wait()
+
+        bias = 8 * n_pp + 2 * n_layer + shift + 4 + spacing
         bias = spacing * (-(-bias // spacing))
         turn = {}
         for name, start in (("f", f_start), ("b", b_start)):
@@ -288,13 +351,18 @@
                 ok = ok & extra
             pl.when(ok)(lambda: fn(layer, m))
 
-        at("b", 3, bwd_b, 0, s > 0)
+        here, host, far = s < away, s == host_stage, 4 * (last - host_stage)
+        at("b", 3, bwd_b, 0, here & (s > 0))
+        at("b", 3 - far, bwd_b_guest, 0, host)
         at("b", 2, bwd_a, 0)
-        at("b", 1, bwd_b, 1)
+        at("b", 1, bwd_b, 1, here)
+        at("b", 1 - far, bwd_b_guest, 1, host)
         at("b", 0, bwd_a, 1)
-        at("f", 3, fwd_b, 1)
+        at("f", 3, fwd_b, 1, here)
+        at("f", 3 + far, fwd_b_guest, 1, host)
         at("f", 2, fwd_a, 1)
-        at("f", 1, fwd_b, 0)
+        at("f", 1, fwd_b, 0, here)
+        at("f", 1 + far, fwd_b_guest, 0, host)
         at("f", 0, fwd_a, 0)
         return carry
 
@@ -313,25 +381,82 @@
 
     for lp in (0, 1, 3):
         wait_three(rs_ssem.at[lp])
-    wait_three(ag_ssem.at[0])
-    wait_three(ag_ssem.at[3])
-
-    @pl.when(s < last)
-    def _():
+
+    @pl.when(s < away)
+    def _():
+        wait_three(ag_ssem.at[0])
+        wait_three(ag_ssem.at[3])
         wait_four(ag_ssem.at[1])
 
-    @pl.when(s == last)
-    def _():
-        wait_three(ag_ssem.at[1])
-        pltpu.make_async_copy(loss_all.at[0:3], loss_all.at[0:3], loss_ssem.at[0]).wait()
+    @pl.when((s < away) & (s > 0))
+    def _():
+        wait_four(ag_ssem.at[2])
+
+    @pl.when(s >= away)
+    def _():
+        for lp in range(4):
+            pltpu.make_async_copy(own_send.at[lp], own_send.at[lp], own_ssem.at[lp]).wait()
+
+    @pl.when(s == host_stage)
+    def _():
+        for lp in range(4):
+            wait_four(guest_ssem.at[lp])
+
+    @pl.when(s == host_stage)
+    def _():
+        pltpu.make_async_copy(loss_all, loss_all, loss_ssem.at[0]).wait()
 
     @pl.when(s > 0)
     def _():
         wait_three(rs_ssem.at[2])
-        wait_four(ag_ssem.at[2])
         pltpu.make_async_copy(loss_tot, loss_tot, loss_ssem.at[1]).wait()
 
     loss_out[...] = loss_tot[...]
+
+
+def dot_tokens(a, b):
+    return lax.dot_general(a, b, (((0,), (0,)), ((), ())), preferred_element_type=F32)
+
+
+def grad_kernel(inv_count, a_ref, g_ref, z_ref, dh_ref, loss_ref, first_ref, second_ref, total_ref):
+    @pl.when((pl.program_id(0) == 0) & (pl.program_id(1) == 0))
+    def _():
+        total_ref[0, 0] = jnp.sum(loss_ref[...]) * inv_count
+
+    first_ref[0] = dot_tokens(a_ref[0], g_ref[0])
+    second_ref[0] = dot_tokens(z_ref[0], dh_ref[0])
+
+
+def weight_grads(a, g, z, dh, loss, inv_count):
+    n_layer, n_tok, d_model = a.shape
+    hidden = g.shape[2]
+    steps = d_model // GRAD_TILE
+    rows2 = hidden // steps
+    return pl.pallas_call(
+        functools.partial(grad_kernel, inv_count),
+        grid=(n_layer, steps),
+        in_specs=[
+            pl.BlockSpec((1, n_tok, GRAD_TILE), lambda l, j: (l, 0, j)),
+            pl.BlockSpec((1, n_tok, hidden), lambda l, j: (l, 0, 0)),
+            pl.BlockSpec((1, n_tok, rows2), lambda l, j: (l, 0, j)),
+            pl.BlockSpec((1, n_tok, d_model), lambda l, j: (l, 0, 0)),
+            pl.BlockSpec((8, 128), lambda l, j: (0, 0)),
+        ],
+        out_specs=[
+            pl.BlockSpec((1, GRAD_TILE, hidden), lambda l, j: (l, j, 0)),
+            pl.BlockSpec((1, rows2, d_model), lambda l, j: (l, j, 0)),
+            pl.BlockSpec(memory_space=pltpu.SMEM),
+        ],
+        out_shape=[
+            jax.ShapeDtypeStruct((n_layer, d_model, hidden), F32),
+            jax.ShapeDtypeStruct((n_layer, hidden, d_model), F32),
+            jax.ShapeDtypeStruct((1, 1), F32),
+        ],
+        compiler_params=pltpu.CompilerParams(vmem_limit_bytes=63 * 1024 * 1024),
+        cost_estimate=pl.CostEstimate(
+            flops=8 * n_tok * d_model * hidden, bytes_accessed=4 * n_layer * 2 * n_tok * d_model * 2, transcendentals=0),
+        name="weight_grads",
+    )(a, g, z, dh, loss)
 
 
 def solution(mesh):
@@ -376,24 +501,30 @@
                 pltpu.VMEM((8, 128), F32),
                 pltpu.VMEM((n_tp, 8, 128), F32),
                 pltpu.VMEM((8, 128), F32),
+                pltpu.VMEM((4, 3, n_tok, ds), BF16),
+                pltpu.VMEM((4, n_tok, ds), F32),
+                pltpu.VMEM((4, n_tok, ds), F32),
+                pltpu.VMEM((4, n_tok, ds), BF16),
                 dma((3 + 3 * n_tp,)),
                 dma((4, 3, n_mb)),
                 dma((4, n_tp, n_mb)),
                 dma((4,)),
                 dma((4,)),
                 dma((8,)),
+                dma((4, 4, n_mb)),
+                dma((4,)),
+                dma((4,)),
                 dma((n_tp,)),
                 dma,
                 dma((2,)),
             ],
-            compiler_params=pltpu.CompilerParams(has_side_effects=True, vmem_limit_bytes=60 * 1024 * 1024),
+            compiler_params=pltpu.CompilerParams(has_side_effects=True, vmem_limit_bytes=63 * 1024 * 1024),
             cost_estimate=pl.CostEstimate(flops=10**11, bytes_accessed=10**8, transcendentals=0),
             name="mlp_stack",
         )(x_loc.reshape(n_tok, d_model), y_loc.reshape(n_tok, d_model), w_in[0], w_out[0])
-        grad_first = jnp.einsum("ltd,ltf->ldf", a, g, preferred_element_type=F32)[None]
-        grad_second = jnp.einsum("ltf,ltd->lfd", z, dh, preferred_element_type=F32)[None]
-        loss_val = (jnp.sum(loss) * inv_count).reshape(1)
-        return grad_first, grad_second, loss_val
+        grad_first, grad_second, loss_val = weight_grads(a, g, z, dh, loss, inv_count)
+        grad_first, grad_second = grad_first[None], grad_second[None]
+        return grad_first, grad_second, loss_val.reshape(1)
 
     return jax.shard_map(
         device_program,

time: 482 us -> 465 us (0.965)
  matrix products: 18.4 us -> 0 us
    dot_general x2 -> x0, matrix products: 18.4 us -> none  [the longest x1 11.6 us: device_program(): jnp.einsum('ltd,ltf->ldf', a, g, preferred_element_type=F32)[None]]
    pallas_call x0 -> x1, Pallas kernels: none -> 16.6 us  [weight_grads(): pl.pallas_call(functools.partial(grad_kernel, inv_count), grid=(n_layer,...]
    pallas_call x1, Pallas kernels: 460 us -> 447 us  [device_program(): pl.pallas_call(kernel, out_shape=[jax.ShapeDtypeStruct((2, n_tok, d_model...]
where the time goes in v3:
time: 465 us; the launch traced here: 464 us
  Pallas kernels  464 us (100%)
    pallas_call x1, Pallas kernels, device_program(): pl.pallas_call(kernel, out_shape=[jax.ShapeDtypeStruct((2, n_tok, d_model...  447 us
    pallas_call x1, Pallas kernels, weight_grads(): pl.pallas_call(functools.partial(grad_kernel, inv_count), grid=(n_layer,...  16.6 us

profile of v3, /device:TPU:96, one launch (start us, length us, event | category | flops | bytes accessed | tf_op | source)
XLA Modules:
  0.0 464.4 jit_solution(1064754842402937776)
XLA Ops:
  0.6 447.2 %mlp_stack.1 = (bf16[2,1024,1024]{2,1,0:T(8,128)(2,1)}, bf16[2,1024,1024]{2,1,0:T(8,128)(2,1)}, bf16[2,1024,1024]{2,1,0:T(8,128)(2,1)}, bf16[2,1024,1024]{2,1,0:T(8,128)(2,1)}, f32[8,128]{1,0:T(8,128)}) custom-call(bf16[1024,1024]{1,0:T(8,128)(2,1)} %bitcast.9, bf16[1024,1024]{1,0:T(8,128)(2,1)} %bitcast.10, bf16[2,1024,1024]{2,1,0:T(8,128)(2,1)} %bitcast.7, ...), custom_call_target="tpu_custom_call" | custom-call | flops 99999997952 | bytes 100000000 | tf_op jit(solution)/shard_map/mlp_stack/pallas_call | solution.py:477
  447.8 16.6 %weight_grads.1 = (f32[2,1024,1024]{2,1,0:T(8,128)}, f32[2,1024,1024]{2,1,0:T(8,128)}, f32[1,1]{1,0:T(1,128)}) custom-call(bf16[2,1024,1024]{2,1,0:T(8,128)(2,1)} %get-tuple-element.11.a_ref, bf16[2,1024,1024]{2,1,0:T(8,128)(2,1)} %get-tuple-element.12.g_ref, bf16[2,1024,1024]{2,1,0:T(8,128)(2,1)} %get-tuple-element.13.z_ref, ...), custom_call_target="tpu_custom_call" | custom-call | flops 8589934592 | bytes 33554432 | tf_op jit(solution)/shard_map/weight_grads/pallas_call | solution.py:435

commit v4 on v3

--- a/solution.py
+++ b/solution.py
@@ -42,7 +42,7 @@
                  a_out, dh_out, z_out, g_out, loss_out,
                  w1, w2, a_buf, dh_buf, u_buf, z_buf, g_buf, rs_recv, rs_send, hs_send,
                  own_part, t_buf, loss_acc, loss_all, loss_tot,
-                 guest_recv, guest_own, own_send, guest_send,
+                 guest_own, own_send, guest_send,
                  load_sem, rs_rsem, ag_rsem, rs_ssem, ag_ssem, out_sem,
                  guest_rsem, guest_ssem, own_ssem,
                  lall_rsem, ltot_rsem, loss_ssem):
@@ -56,7 +56,7 @@
     hidden = w1.shape[2]
     n_mb = n_tok // rows_mb
     n_layer = 2 * n_pp
-    hc = 256
+    hc = 512
 
     def peer(d):
         return lax.rem(t + d, n_tp)
@@ -69,34 +69,38 @@
         for j in range(n_tp):
             loads[layer].append(pltpu.make_async_copy(
                 w2_hbm.at[layer, :, pl.ds(j * ds, ds)], w2.at[layer, j], load_sem.at[2 + layer * n_tp + j]))
-    x_loads = [pltpu.make_async_copy(x_hbm.at[:, pl.ds(j * ds, ds)], a_buf.at[0, j], load_sem.at[2 + 2 * n_tp + j])
-               for j in range(n_tp)]
-    y_load = pltpu.make_async_copy(y_hbm.at[:, pl.ds(pl.multiple_of(t * ds, ds), ds)], t_buf, load_sem.at[2 + 3 * n_tp])
+    def x_load(j, first, rows, sem):
+        return pltpu.make_async_copy(
+            x_hbm.at[pl.ds(first, rows), pl.ds(j * ds, ds)], a_buf.at[0, j, pl.ds(first, rows)], load_sem.at[sem + j])
+
+    x_head = [x_load(j, 0, rows_mb, 2 + 2 * n_tp) for j in range(n_tp)]
+    x_tail = [x_load(j, rows_mb, n_tok - rows_mb, 2 + 3 * n_tp) for j in range(n_tp)]
+    y_load = pltpu.make_async_copy(
+        y_hbm.at[:, pl.ds(pl.multiple_of(t * ds, ds), ds)], t_buf, load_sem.at[2 + 4 * n_tp])
 
     @pl.when(s == 0)
     def _():
-        for c in x_loads:
+        for c in x_head:
             c.start()
 
-    for c in loads[0] + loads[1]:
+    for c in loads[0]:
         c.start()
 
     @pl.when(s == host_stage)
     def _():
-        y_load.start()
         loss_acc[...] = jnp.zeros_like(loss_acc)
 
     @pl.when(s == 0)
     def _():
-        for c in x_loads:
+        for c in x_head:
             c.wait()
 
     for c in loads[0]:
         c.wait()
-
-    @pl.when(s == host_stage)
-    def _():
-        y_load.wait()
+    for c in loads[1]:
+        c.start()
+    pl.when(s == 0)(lambda: [c.start() for c in x_tail] and None)
+    pl.when(s == host_stage)(y_load.start)
 
     def rows_of(m):
         return pl.ds(pl.multiple_of(m * rows_mb, rows_mb), rows_mb)
@@ -113,22 +117,15 @@
         for j in range(n_tp):
             pltpu.make_async_copy(buf.at[layer, j, rows], out.at[layer, rows, pl.ds(j * ds, ds)], sem).start()
 
+    moved = lax.div(s, last)
+    reducer = s + moved * (host_stage - last)
+
     def send_part(lp, d, m):
         rows = rows_of(m)
-
-        @pl.when(s < away)
-        def _():
-            pltpu.make_async_remote_copy(
-                src_ref=rs_send.at[lp, d - 1, rows], dst_ref=rs_recv.at[lp, d - 1, rows],
-                send_sem=rs_ssem.at[lp], recv_sem=rs_rsem.at[lp, d - 1, m],
-                device_id={"pp": s, "tp": peer(d)}, device_id_type=pl.DeviceIdType.MESH).start()
-
-        @pl.when(s >= away)
-        def _():
-            pltpu.make_async_remote_copy(
-                src_ref=rs_send.at[lp, d - 1, rows], dst_ref=guest_recv.at[lp, d - 1, rows],
-                send_sem=rs_ssem.at[lp], recv_sem=guest_rsem.at[lp, d - 1, m],
-                device_id={"pp": host_stage, "tp": peer(d)}, device_id_type=pl.DeviceIdType.MESH).start()
+        pltpu.make_async_remote_copy(
+            src_ref=rs_send.at[lp, d - 1, rows], dst_ref=rs_recv.at[moved, lp, d - 1, rows],
+            send_sem=rs_ssem.at[lp], recv_sem=rs_rsem.at[moved, lp, d - 1, m],
+            device_id={"pp": reducer, "tp": peer(d)}, device_id_type=pl.DeviceIdType.MESH).start()
 
     def send_slice(lp, buf, layer, lp_dst, stage, d, m):
         rows = rows_of(m)
@@ -145,10 +142,11 @@
                 send_sem=guest_ssem.at[lp], recv_sem=ag_rsem.at[lp_dst, t, m],
                 device_id={"pp": stage, "tp": peer(d)}, device_id_type=pl.DeviceIdType.MESH).start()
 
-    def partials(lp, m, buf, layer, fn):
+    def partials(lp, m, buf, layer, farthest, fn):
         rows = rows_of(m)
         for d in far_first:
-            rs_send[lp, d - 1, rows, :] = fn(peer(d)).astype(BF16)
+            part = farthest if d == far_first[0] else fn(peer(d))
+            rs_send[lp, d - 1, rows, :] = part.astype(BF16)
             send_part(lp, d, m)
         own = buf[layer, t, rows, :].astype(F32) + fn(t)
 
@@ -161,29 +159,29 @@
             own_send[lp, rows, :] = own
             pltpu.make_async_remote_copy(
                 src_ref=own_send.at[lp, rows], dst_ref=guest_own.at[lp, rows],
-                send_sem=own_ssem.at[lp], recv_sem=guest_rsem.at[lp, 3, m],
+                send_sem=own_ssem.at[lp], recv_sem=guest_rsem.at[lp, m],
                 device_id={"pp": host_stage, "tp": t}, device_id_type=pl.DeviceIdType.MESH).start()
 
     def reduce_own(lp, m):
         rows = rows_of(m)
         for d in (1, 3, 2):
-            ref = rs_recv.at[lp, d - 1, rows]
-            pltpu.make_async_copy(ref, ref, rs_rsem.at[lp, d - 1, m]).wait()
+            ref = rs_recv.at[0, lp, d - 1, rows]
+            pltpu.make_async_copy(ref, ref, rs_rsem.at[0, lp, d - 1, m]).wait()
         acc = own_part[lp]
         for d in (1, 3, 2):
-            acc = acc + rs_recv[lp, d - 1, rows, :].astype(F32)
+            acc = acc + rs_recv[0, lp, d - 1, rows, :].astype(F32)
         return acc.astype(BF16)
 
     def reduce_guest(lp, m):
         rows = rows_of(m)
         for d in (1, 3, 2):
-            ref = guest_recv.at[lp, d - 1, rows]
-            pltpu.make_async_copy(ref, ref, guest_rsem.at[lp, d - 1, m]).wait()
+            ref = rs_recv.at[1, lp, d - 1, rows]
+            pltpu.make_async_copy(ref, ref, rs_rsem.at[1, lp, d - 1, m]).wait()
         ref = guest_own.at[lp, rows]
-        pltpu.make_async_copy(ref, ref, guest_rsem.at[lp, 3, m]).wait()
+        pltpu.make_async_copy(ref, ref, guest_rsem.at[lp, m]).wait()
         acc = guest_own[lp, rows, :]
         for d in (1, 3, 2):
-            acc = acc + guest_recv[lp, d - 1, rows, :].astype(F32)
+            acc = acc + rs_recv[1, lp, d - 1, rows, :].astype(F32)
         return acc.astype(BF16)
 
     def fwd_a(layer, m):
@@ -207,8 +205,11 @@
                 acc = acc + dot(a_buf[layer, j, rows, :], w1[layer, j * ds:(j + 1) * ds, cols])
             u = acc.astype(BF16)
             u_buf[layer, rows, cols] = u
-            z_buf[layer, rows, cols] = gelu_fwd(u.astype(F32)).astype(BF16)
-        partials(layer, m, a_buf, layer, lambda j: dot(z_buf[layer, rows, :], w2[layer, j]))
+            z = gelu_fwd(u.astype(F32)).astype(BF16)
+            z_buf[layer, rows, cols] = z
+            part = dot(z, w2[layer, peer(far_first[0]), cols, :])
+            farthest = part if c == 0 else farthest + part
+        partials(layer, m, a_buf, layer, farthest, lambda j: dot(z_buf[layer, rows, :], w2[layer, j]))
         copy_out_slices(a_buf, a_out, layer, m, out_sem.at[layer])
         pltpu.make_async_copy(z_buf.at[layer, rows], z_out.at[layer, rows], out_sem.at[4 + layer]).start()
 
@@ -282,16 +283,20 @@
             @pl.when(s >= away)
             def _():
                 wait_slices(dh_buf, 0, 2, m, True)
+        far_rows = pl.ds(pl.multiple_of(peer(far_first[0]) * ds, ds), ds)
         for c in range(hidden // hc):
             cols = slice(c * hc, (c + 1) * hc)
             acc = dot_t(dh_buf[layer, 0, rows, :], w2[layer, 0, cols, :])
             for j in range(1, n_tp):
                 acc = acc + dot_t(dh_buf[layer, j, rows, :], w2[layer, j, cols, :])
             u = u_buf[layer, rows, cols].astype(F32)
-            g_buf[layer, rows, cols] = (gelu_grad(u) * acc).astype(BF16)
+            g = (gelu_grad(u) * acc).astype(BF16)
+            g_buf[layer, rows, cols] = g
+            part = dot_t(g, w1[layer, far_rows, cols])
+            farthest = part if c == 0 else farthest + part
 
         def send():
-            partials(lp, m, dh_buf, layer, lambda j: dot_t(
+            partials(lp, m, dh_buf, layer, farthest, lambda j: dot_t(
                 g_buf[layer, rows, :], w1[layer, pl.ds(pl.multiple_of(j * ds, ds), ds), :]))
 
         if layer == 1:
@@ -333,6 +338,15 @@
         def _():
             for c in loads[1]:
                 c.wait()
+
+        @pl.when((k == 1) & (s == 0))
+        def _():
+            for c in x_tail:
+                c.wait()
+
+        @pl.when((k == 1) & (s == host_stage))
+        def _():
+            y_load.wait()
 
         bias = 8 * n_pp + 2 * n_layer + shift + 4 + spacing
         bias = spacing * (-(-bias // spacing))
@@ -493,7 +507,7 @@
                 pltpu.VMEM((2, n_tok, hidden), BF16),
                 pltpu.VMEM((2, n_tok, hidden), BF16),
                 pltpu.VMEM((2, n_tok, hidden), BF16),
-                pltpu.VMEM((4, 3, n_tok, ds), BF16),
+                pltpu.VMEM((2, 4, 3, n_tok, ds), BF16),
                 pltpu.VMEM((4, 3, n_tok, ds), BF16),
                 pltpu.VMEM((4, n_tok, ds), BF16),
                 pltpu.VMEM((4, rows_mb, ds), F32),
@@ -501,17 +515,16 @@
                 pltpu.VMEM((8, 128), F32),
                 pltpu.VMEM((n_tp, 8, 128), F32),
                 pltpu.VMEM((8, 128), F32),
-                pltpu.VMEM((4, 3, n_tok, ds), BF16),
                 pltpu.VMEM((4, n_tok, ds), F32),
                 pltpu.VMEM((4, n_tok, ds), F32),
                 pltpu.VMEM((4, n_tok, ds), BF16),
-                dma((3 + 3 * n_tp,)),
-                dma((4, 3, n_mb)),
+                dma((3 + 4 * n_tp,)),
+                dma((2, 4, 3, n_mb)),
                 dma((4, n_tp, n_mb)),
                 dma((4,)),
                 dma((4,)),
                 dma((8,)),
-                dma((4, 4, n_mb)),
+                dma((4, n_mb)),
                 dma((4,)),
                 dma((4,)),
                 dma((n_tp,)),

time: 465 us -> 461 us (level)
  no operation moved by 1% of the time
where the time goes in v4:
time: 461 us; the launch traced here: 460 us
  Pallas kernels  460 us (100%)
    pallas_call x1, Pallas kernels, device_program(): pl.pallas_call(kernel, out_shape=[jax.ShapeDtypeStruct((2, n_tok, d_model...  443 us
    pallas_call x1, Pallas kernels, weight_grads(): pl.pallas_call(functools.partial(grad_kernel, inv_count), grid=(n_layer,...  16.6 us

profile of v4, /device:TPU:96, one launch (start us, length us, event | category | flops | bytes accessed | tf_op | source)
XLA Modules:
  0.0 460.5 jit_solution(4215407405701283548)
XLA Ops:
  0.6 443.2 %mlp_stack.1 = (bf16[2,1024,1024]{2,1,0:T(8,128)(2,1)}, bf16[2,1024,1024]{2,1,0:T(8,128)(2,1)}, bf16[2,1024,1024]{2,1,0:T(8,128)(2,1)}, bf16[2,1024,1024]{2,1,0:T(8,128)(2,1)}, f32[8,128]{1,0:T(8,128)}) custom-call(bf16[1024,1024]{1,0:T(8,128)(2,1)} %bitcast.9, bf16[1024,1024]{1,0:T(8,128)(2,1)} %bitcast.10, bf16[2,1024,1024]{2,1,0:T(8,128)(2,1)} %bitcast.7, ...), custom_call_target="tpu_custom_call" | custom-call | flops 99999997952 | bytes 100000000 | tf_op jit(solution)/shard_map/mlp_stack/pallas_call | solution.py:491
  443.8 16.6 %weight_grads.1 = (f32[2,1024,1024]{2,1,0:T(8,128)}, f32[2,1024,1024]{2,1,0:T(8,128)}, f32[1,1]{1,0:T(1,128)}) custom-call(bf16[2,1024,1024]{2,1,0:T(8,128)(2,1)} %get-tuple-element.11.a_ref, bf16[2,1024,1024]{2,1,0:T(8,128)(2,1)} %get-tuple-element.12.g_ref, bf16[2,1024,1024]{2,1,0:T(8,128)(2,1)} %get-tuple-element.13.z_ref, ...), custom_call_target="tpu_custom_call" | custom-call | flops 8589934592 | bytes 33554432 | tf_op jit(solution)/shard_map/weight_grads/pallas_call | solution.py:449

commit v5 on v4

--- a/solution.py
+++ b/solution.py
@@ -40,7 +40,7 @@
 def stack_kernel(n_pp, n_tp, rows_mb, spacing, shift, inv_count,
                  x_hbm, y_hbm, w1_hbm, w2_hbm,
                  a_out, dh_out, z_out, g_out, loss_out,
-                 w1, w2, a_buf, dh_buf, u_buf, z_buf, g_buf, rs_recv, rs_send, hs_send,
+                 w1, w2, a_buf, dh_buf, slope_buf, z_buf, g_buf, rs_recv, rs_send, hs_send,
                  own_part, t_buf, loss_acc, loss_all, loss_tot,
                  guest_own, own_send, guest_send,
                  load_sem, rs_rsem, ag_rsem, rs_ssem, ag_ssem, out_sem,
@@ -204,12 +204,13 @@
             for j in range(1, n_tp):
                 acc = acc + dot(a_buf[layer, j, rows, :], w1[layer, j * ds:(j + 1) * ds, cols])
             u = acc.astype(BF16)
-            u_buf[layer, rows, cols] = u
+            g_buf[layer, rows, cols] = u
             z = gelu_fwd(u.astype(F32)).astype(BF16)
             z_buf[layer, rows, cols] = z
             part = dot(z, w2[layer, peer(far_first[0]), cols, :])
             farthest = part if c == 0 else farthest + part
         partials(layer, m, a_buf, layer, farthest, lambda j: dot(z_buf[layer, rows, :], w2[layer, j]))
+        slope_buf[layer, rows, :] = gelu_grad(g_buf[layer, rows, :].astype(F32))
         copy_out_slices(a_buf, a_out, layer, m, out_sem.at[layer])
         pltpu.make_async_copy(z_buf.at[layer, rows], z_out.at[layer, rows], out_sem.at[4 + layer]).start()
 
@@ -289,8 +290,7 @@
             acc = dot_t(dh_buf[layer, 0, rows, :], w2[layer, 0, cols, :])
             for j in range(1, n_tp):
                 acc = acc + dot_t(dh_buf[layer, j, rows, :], w2[layer, j, cols, :])
-            u = u_buf[layer, rows, cols].astype(F32)
-            g = (gelu_grad(u) * acc).astype(BF16)
+            g = (slope_buf[layer, rows, cols] * acc).astype(BF16)
             g_buf[layer, rows, cols] = g
             part = dot_t(g, w1[layer, far_rows, cols])
             farthest = part if c == 0 else farthest + part
@@ -504,7 +504,7 @@
                 pltpu.VMEM((2, n_tp, hidden, ds), BF16),
                 pltpu.VMEM((2, n_tp, n_tok, ds), BF16),
                 pltpu.VMEM((2, n_tp, n_tok, ds), BF16),
-                pltpu.VMEM((2, n_tok, hidden), BF16),
+                pltpu.VMEM((2, n_tok, hidden), F32),
                 pltpu.VMEM((2, n_tok, hidden), BF16),
                 pltpu.VMEM((2, n_tok, hidden), BF16),
                 pltpu.VMEM((2, 4, 3, n_tok, ds), BF16),
@@ -531,7 +531,7 @@
                 dma,
                 dma((2,)),
             ],
-            compiler_params=pltpu.CompilerParams(has_side_effects=True, vmem_limit_bytes=63 * 1024 * 1024),
+            compiler_params=pltpu.CompilerParams(has_side_effects=True, vmem_limit_bytes=67043328),
             cost_estimate=pl.CostEstimate(flops=10**11, bytes_accessed=10**8, transcendentals=0),
             name="mlp_stack",
         )(x_loc.reshape(n_tok, d_model), y_loc.reshape(n_tok, d_model), w_in[0], w_out[0])

time: 461 us -> 465 us (level)
  no operation moved by 1% of the time
where the time goes in v5:
time: 465 us; the launch traced here: 464 us
  Pallas kernels  464 us (100%)
    pallas_call x1, Pallas kernels, device_program(): pl.pallas_call(kernel, out_shape=[jax.ShapeDtypeStruct((2, n_tok, d_model...  447 us
    pallas_call x1, Pallas kernels, weight_grads(): pl.pallas_call(functools.partial(grad_kernel, inv_count), grid=(n_layer,...  16.6 us

profile of v5, /device:TPU:96, one launch (start us, length us, event | category | flops | bytes accessed | tf_op | source)
XLA Modules:
  0.0 464.5 jit_solution(3003534245887222124)
XLA Ops:
  0.6 447.2 %mlp_stack.1 = (bf16[2,1024,1024]{2,1,0:T(8,128)(2,1)}, bf16[2,1024,1024]{2,1,0:T(8,128)(2,1)}, bf16[2,1024,1024]{2,1,0:T(8,128)(2,1)}, bf16[2,1024,1024]{2,1,0:T(8,128)(2,1)}, f32[8,128]{1,0:T(8,128)}) custom-call(bf16[1024,1024]{1,0:T(8,128)(2,1)} %bitcast.9, bf16[1024,1024]{1,0:T(8,128)(2,1)} %bitcast.10, bf16[2,1024,1024]{2,1,0:T(8,128)(2,1)} %bitcast.7, ...), custom_call_target="tpu_custom_call" | custom-call | flops 99999997952 | bytes 100000000 | tf_op jit(solution)/shard_map/mlp_stack/pallas_call | solution.py:491
  447.8 16.6 %weight_grads.1 = (f32[2,1024,1024]{2,1,0:T(8,128)}, f32[2,1024,1024]{2,1,0:T(8,128)}, f32[1,1]{1,0:T(1,128)}) custom-call(bf16[2,1024,1024]{2,1,0:T(8,128)(2,1)} %get-tuple-element.11.a_ref, bf16[2,1024,1024]{2,1,0:T(8,128)(2,1)} %get-tuple-element.12.g_ref, bf16[2,1024,1024]{2,1,0:T(8,128)(2,1)} %get-tuple-element.13.z_ref, ...), custom_call_target="tpu_custom_call" | custom-call | flops 8589934592 | bytes 33554432 | tf_op jit(solution)/shard_map/weight_grads/pallas_call | solution.py:449
